TPU v7x, 32 devices: a whole 2x2x4 slice. The times are simulated.
32 devices in a mesh: gx: 8 (over y, x, core), gy: 4 (over z).
Axes of the slice: x: 2, y: 2, z: 4, core: 2. Of those that a mesh axis runs over, the one named last changes fastest.
Arguments:
- features: bfloat16 [8, 4, 128, 128], P('gx', 'gy'), may hold values from -6 to 6
- offsets: float32 [8, 4, 3, 128], P('gx', 'gy'), may hold values from 0 to 1
- counts: int32 [8, 4, 4], P('gx', 'gy'), may hold values from 1 to 32, as said below
- wave_index: int32 [3, 512], replicated, may hold values from -5 to 5, as said below
- screening: float32 [2, 128], replicated, may hold values from 1 to 8
- charge_weight: bfloat16 [2, 128, 128], replicated, may hold values from -0.5 to 0.5
- ewald_weight: bfloat16 [2, 128, 128], replicated, may hold values from -0.5 to 0.5
- input_weight: bfloat16 [2, 128, 128], replicated, may hold values from -0.5 to 0.5
- filter_weight: bfloat16 [2, 128, 128], replicated, may hold values from -0.5 to 0.5
- middle_weight: bfloat16 [2, 128, 128], replicated, may hold values from -0.5 to 0.5
- output_weight: bfloat16 [2, 128, 128], replicated, may hold values from -0.5 to 0.5
Outputs:
- updated: bfloat16 [8, 4, 128, 128], P('gx', 'gy')
Inputs may be any that keep to these rules, and one draw needn't show every extreme that they name: `counts`: atoms in a cell; some cell of every draw is full. `wave_index`: integer wave numbers; the 512 vectors are distinct, none is zero, and no two are opposite.
All inputs are finite; a program needn't handle non-finite values.
Results may differ from a plain program's by a relative error of at most 0.007.
Values may be sent and summed in bfloat16 or wider, within the bound.
No kernel may reach another device: no remote copies, remote signals or barrier semaphores. Data moves between devices by JAX's collectives and lax.ppermute only.
A program may use at most 64 MiB of HBM per device.

v0:
```python
import functools
import math

import jax
import jax.numpy as jnp
from jax import lax
from jax.experimental import pallas as pl
from jax.experimental.pallas import tpu as pltpu
from jax.sharding import PartitionSpec as P


f32 = jnp.float32
bf16 = jnp.bfloat16

LANES = 128
PARTS = 3
GEO = 16
LIVE, SPOT_X, SPOT_Y, LAYER, SLOT = 9, 10, 11, 12, 13
CHUNK = 256
GROUP = 16
NONE = -1.0e30

COS_TURN = (
    1.0,
    -19.73920440673828,
    64.93911743164062,
    -85.45011138916016,
    60.16743087768555,
    -25.96688461303711,
    6.527706146240234,
)
SIN_TURN = (
    6.2831854820251465,
    -41.34170150756836,
    81.60513305664062,
    -76.7030029296875,
    42.02585220336914,
    -14.899578094482422,
    3.2377800941467285,
)
COS_HALF = (
    1.0,
    -1.2337005138397217,
    0.2536693215370178,
    -0.02086268737912178,
    0.000917722936719656,
    -2.3824151867302135e-05,
)


def power_sum(terms, x):
    out = terms[-1] * x + terms[-2]
    for term in terms[-3::-1]:
        out = out * x + term
    return out


def mm(a, b):
    return jnp.dot(a, b, preferred_element_type=f32)


def mm_nt(a, b):
    return lax.dot_general(a, b, (((1,), (1,)), ((), ())), preferred_element_type=f32)


def mm_tn(a, b):
    return lax.dot_general(a, b, (((0,), (0,)), ((), ())), preferred_element_type=f32)


def silu(t):
    return t / (1.0 + jnp.exp(-t))


def iota(shape, dim):
    return lax.broadcasted_iota(jnp.int32, shape, dim)


def vmem():
    return pl.BlockSpec(memory_space=pltpu.VMEM)


def smem():
    return pl.BlockSpec(memory_space=pltpu.SMEM)


def pack_kernel(counts_ref, features_ref, offsets_ref, out_ref):
    depth = counts_ref.shape[2]
    atoms, _ = features_ref.shape[2:]
    slots = atoms // depth
    out_ref[0:atoms, :] = features_ref[0, 0]
    rows = []
    for axis in range(3):
        rest = offsets_ref[0, 0, axis : axis + 1, :]
        for _ in range(PARTS):
            piece = rest.astype(bf16).astype(f32)
            rows.append(piece)
            rest = rest - piece
    lane = iota((1, atoms), 1)
    limit = jnp.zeros((1, atoms), jnp.int32)
    for cell in range(depth):
        limit = jnp.where(lane // slots == cell, counts_ref[0, 0, cell], limit)
    rows.append((lane - (lane // slots) * slots < limit).astype(f32))
    rows.append(jnp.full((1, atoms), lax.axis_index("gx"), jnp.int32).astype(f32))
    rows.append(jnp.full((1, atoms), lax.axis_index("gy"), jnp.int32).astype(f32))
    rows.append((lane // slots).astype(f32))
    rows.append((lane + 1).astype(f32))
    rows.append(jnp.zeros((GEO - len(rows), atoms), f32))
    out_ref[atoms : atoms + GEO, :] = jnp.concatenate(rows, axis=0).astype(bf16)


def places(live, span):
    rows, atoms = live.shape
    before = (iota((atoms, atoms), 0) < iota((atoms, atoms), 1)).astype(f32).astype(bf16)
    live_b = live.astype(bf16)
    inside = mm(live_b, before)
    total = mm(live_b, jnp.ones((atoms, atoms), bf16))
    row, other = iota((rows, rows), 0), iota((rows, rows), 1)
    above = jnp.logical_and(other < row, other // span == row // span).astype(f32).astype(bf16)
    return jnp.where(live > 0.0, inside + mm(above, total.astype(bf16)), -1.0)


def chosen(place, first, size):
    want = (iota((size, place.shape[1]), 0) + first).astype(f32)
    return jnp.concatenate(
        [jnp.where(want == place[c : c + 1, :], 1.0, 0.0).astype(bf16) for c in range(place.shape[0])],
        axis=1,
    )


def identity(rows, columns):
    return (iota((rows, columns), 0) == iota((rows, columns), 1)).astype(f32).astype(bf16)


def joined(known, axis):
    parts = [known[PARTS * axis + p : PARTS * axis + p + 1] for p in range(PARTS)]
    return (parts[0] + parts[1]) + parts[2]


def grouped(known, groups):
    out = known[0:GEO]
    for g in range(1, groups):
        out = out + known[g * GEO : (g + 1) * GEO]
    return out


def wrapped(step, size):
    step = jnp.where(step > 0.5 * size, step - size, step)
    return jnp.where(step < -0.5 * size, step + size, step)


def outside(x):
    return jnp.maximum(jnp.maximum(-x, x - 1.0), 0.0)


def conv_kernel(
    depth,
    slots,
    size_x,
    size_y,
    rows_of,
    index,
    geo_a,
    geo_b,
    geo_c,
    state_a,
    state_b,
    state_c,
    input_ref,
    filter_ref,
    middle_ref,
    output_ref,
    out_ref,
    source_ref,
    place_ref,
    scale_ref,
    weight_ref,
    basis_ref,
    wide_ref,
    center_ref,
    message_ref,
    mapped_ref,
):
    atoms, channels = message_ref.shape
    count = filter_ref.shape[1]
    spread = math.sqrt(0.25 * math.log2(math.e))
    geo = (geo_a, geo_b, geo_c)
    state = (state_a, state_b, state_c)
    near = len(rows_of)
    columns = 3 * near
    block = columns + -columns % 8
    eye = identity(atoms, atoms)
    spots = [[], [], [], [], [], []]
    for plane in range(3):
        known = jnp.concatenate([geo[plane][row, atoms : atoms + GEO, :] for row in rows_of], axis=0)
        turned = mm_nt(eye, known)
        group = iota(turned.shape, 1) // GEO
        wide = known.astype(f32)
        if plane == 0:
            here_x = wide[SPOT_X : SPOT_X + 1, 0:1]
            here_y = wide[SPOT_Y : SPOT_Y + 1, 0:1]
            target = [
                (turned[:, PARTS * a : PARTS * a + 1] + turned[:, PARTS * a + 1 : PARTS * a + 2])
                + turned[:, PARTS * a + 2 : PARTS * a + 3]
                for a in range(3)
            ]
        for i, row in enumerate(rows_of):
            part = slice((plane * near + i) * atoms, (plane * near + i + 1) * atoms)
            source_ref[part, 0:channels] = mm(state[plane][row, 0:atoms, :], input_ref[index]).astype(bf16)
            source_ref[part, channels : channels + near * GEO] = jnp.where(group == i, turned, 0.0).astype(bf16)
            own = wide[i * GEO : (i + 1) * GEO]
            for a in range(3):
                spots[a].append(joined(own, a))
            for a, r in ((3, LIVE), (4, SPOT_X), (5, SPOT_Y)):
                spots[a].append(own[r : r + 1])
    fill = [jnp.zeros((block - columns, atoms), f32)]
    x, y, z, live, at_x, at_y = [jnp.concatenate(rows + fill, axis=0) for rows in spots]
    out_x = outside(wrapped(at_x - here_x, size_x) + x)
    out_y = outside(wrapped(at_y - here_y, size_y) + y)
    flat = out_x * out_x + out_y * out_y
    layers = (iota((block, atoms), 1) // slots).astype(f32)
    lives = []
    longest = jnp.int32(0)
    totals = []
    for cell in range(depth):
        out_z = outside(wrapped(layers - float(cell), depth) + z)
        close = jnp.where(flat + out_z * out_z < 1.001, live, 0.0)
        lives.append(close)
        totals.append(jnp.sum(close).astype(jnp.int32))
        longest = jnp.maximum(longest, totals[-1])
    place_ref[...] = places(jnp.concatenate(lives, axis=0), block)
    center_ref[...] = iota((count, CHUNK), 0).astype(f32) * spread
    wide_ref[...] = filter_ref[index].astype(f32)
    message_ref[...] = jnp.zeros_like(message_ref)
    pick_rows = identity(near * GEO, atoms)

    def piece(first, width):
        for cell in range(depth):
            want = chosen(place_ref[cell * block : cell * block + columns, :], first, width)
            found = mm(want, source_ref[...])
            mapped_ref[cell, 0:width, :] = found[:, 0:channels].astype(bf16)
            known = grouped(mm_nt(pick_rows, found[:, channels : 2 * channels].astype(bf16)), near)
            part = slice(cell * slots, (cell + 1) * slots)
            along_x = wrapped(known[SPOT_X : SPOT_X + 1] - here_x, size_x)
            along_y = wrapped(known[SPOT_Y : SPOT_Y + 1] - here_y, size_y)
            along_z = wrapped(known[LAYER : LAYER + 1] - float(cell), depth)
            home = jnp.abs(along_x) + jnp.abs(along_y)
            who = jnp.where(home == 0.0, known[SLOT : SLOT + 1], 0.0)
            diff_x = (along_x + joined(known, 0)) - target[0][part, :]
            diff_y = (along_y + joined(known, 1)) - target[1][part, :]
            diff_z = (along_z + joined(known, 2)) - target[2][part, :]
            square = diff_x * diff_x + diff_y * diff_y + diff_z * diff_z
            dist = jnp.sqrt(square)
            mine = (iota((slots, width), 0) + (cell * slots + 1)).astype(f32)
            kept = jnp.logical_and(dist < 1.0, who != mine)
            kept = jnp.logical_and(kept, iota((slots, width), 1) + first < totals[cell])
            half = jnp.maximum(power_sum(COS_HALF, jnp.minimum(square, 1.0)), 1.0e-18)
            weight_ref[part, 0:width] = jnp.where(kept, 2.0 * jnp.log2(half), NONE)
            scale_ref[part, 0:width] = dist * ((count - 1) * spread)

        def group_step(g, carry):
            start = pl.multiple_of(g * GROUP, GROUP)
            scale = scale_ref[pl.ds(start, GROUP), 0:width]
            weight = weight_ref[pl.ds(start, GROUP), 0:width]
            for i in range(GROUP):
                away = scale[i : i + 1, :] - center_ref[:, 0:width]
                basis_ref[i * count : (i + 1) * count, 0:width] = jnp.exp2(
                    weight[i : i + 1, :] - away * away
                ).astype(bf16)
            sums = mm(basis_ref[:, 0:width], mapped_ref[g // (slots // GROUP), 0:width, :])
            lines = []
            for i in range(GROUP):
                mixed = sums[i * count : (i + 1) * count, :] * wide_ref[...]
                lines.append(jnp.sum(mixed, axis=0, keepdims=True))
            message_ref[pl.ds(start, GROUP), :] += jnp.concatenate(lines, axis=0)
            return carry

        lax.fori_loop(0, atoms // GROUP, group_step, 0)

    full = (longest + (LANES - 1)) // CHUNK

    def chunk_step(chunk, carry):
        piece(chunk * CHUNK, CHUNK)
        return carry

    lax.fori_loop(0, full, chunk_step, 0)

    @pl.when(full * CHUNK < longest)
    def _():
        piece(full * CHUNK, LANES)

    middle = silu(mm(message_ref[...].astype(bf16), middle_ref[index])).astype(bf16)
    out_ref[...] = mm(middle, output_ref[index])


def phase_rows(wave_ref, x, y, z, put):
    waves = wave_ref.shape[1]
    step = 64
    for first in range(0, waves, step):
        part = slice(first, first + step)
        kx, ky, kz = [
            jnp.concatenate([wave_ref[a, part, :]] * (x.shape[1] // LANES), axis=1) for a in range(3)
        ]
        angle = kx * x + ky * y + kz * z
        rest = angle - jnp.round(angle)
        square = rest * rest
        put(first, power_sum(COS_TURN, square).astype(bf16))
        put(waves + first, (power_sum(SIN_TURN, square) * rest).astype(bf16))


def ewald_first(depth, total_atoms, index, wave_ref, screen_ref, geo_ref, *refs):
    ewald_body(depth, total_atoms, index, wave_ref, screen_ref, geo_ref, geo_ref, *refs)


def ewald_body(
    depth,
    total_atoms,
    index,
    wave_ref,
    screen_ref,
    geo_ref,
    state_ref,
    own_ref,
    conv_ref,
    charge_ref,
    update_ref,
    out_ref,
    table_ref,
    own_phase_ref,
    phase_ref,
    factor_ref,
    damp_ref,
    turned_ref,
    place_ref,
    packed_state_ref,
    packed_geo_ref,
    tile_charge_ref,
    tile_spot_ref,
    first_ref,
    number_ref,
):
    planes, columns = geo_ref.shape[0], geo_ref.shape[1]
    atoms, channels = own_ref.shape
    waves = wave_ref.shape[1]
    eye = identity(atoms, atoms)
    numbers = jnp.concatenate([wave_ref[...].astype(f32), jnp.zeros((5, waves), f32)], axis=0).astype(bf16)
    for first in range(0, waves, LANES):
        turned = mm_nt(eye, numbers[:, first : first + LANES])
        for a in range(3):
            table_ref[a, first : first + LANES, :] = jnp.broadcast_to(turned[:, a : a + 1], (LANES, LANES))
    block = columns + -columns % 8

    def plane_live(s, carry):
        lives = [geo_ref[s, t, atoms + LIVE : atoms + LIVE + 1, :].astype(f32) for t in range(columns)]
        if block > columns:
            lives.append(jnp.zeros((block - columns, atoms), f32))
        live = jnp.concatenate(lives, axis=0)
        place_ref[pl.ds(pl.multiple_of(s * block, block), block), :] = live
        known = jnp.concatenate([geo_ref[s, t, atoms : atoms + GEO, :] for t in range(columns)], axis=0)
        if columns * GEO < LANES:
            known = jnp.concatenate([known, jnp.zeros((LANES - columns * GEO, atoms), bf16)], axis=0)
        turned = mm_nt(eye, known)
        group = iota(turned.shape, 1) // GEO
        for t in range(columns):
            turned_ref[s, t * atoms : (t + 1) * atoms, :] = jnp.where(group == t, turned, 0.0).astype(bf16)
        number = jnp.sum(live).astype(jnp.int32)
        number_ref[s] = number
        first_ref[s] = carry[0]
        return carry[0] + number, jnp.maximum(carry[1], number)

    unroll = 8 if planes % 8 == 0 else 1
    total, most = lax.fori_loop(0, planes, plane_live, (jnp.int32(0), jnp.int32(0)), unroll=unroll)
    place_ref[...] = places(place_ref[...], block)
    pairs = (total + (CHUNK - 1)) // CHUNK

    def clear(p, carry):
        packed_state_ref[pl.ds(pl.multiple_of(p * LANES, LANES), LANES), :] = jnp.zeros((LANES, channels), f32)
        packed_geo_ref[pl.ds(pl.multiple_of(p * LANES, LANES), LANES), :] = jnp.zeros((LANES, LANES), f32)
        return carry

    lax.fori_loop(0, 2 * pairs + 2, clear, 0)

    def pick_step(j, carry):
        def plane_step(s, carry):
            start = pl.multiple_of(s * block, block)
            place = place_ref[pl.ds(start, block), :][0:columns]
            want = chosen(place, j * LANES, LANES)
            picked = mm(want, state_ref[s, :, 0:atoms, :].reshape(columns * atoms, channels))
            spots = mm(want, turned_ref[s])

            @pl.when(j * LANES < number_ref[s])
            def _():
                rows = pl.ds(first_ref[s] + j * LANES, LANES)
                packed_state_ref[rows, :] += picked
                packed_geo_ref[rows, :] += spots

            return carry

        return lax.fori_loop(0, planes, plane_step, carry, unroll=unroll)

    lax.fori_loop(0, (most + (LANES - 1)) // LANES, pick_step, 0)

    def places_of(known):
        x = (known[SPOT_X : SPOT_X + 1] + joined(known, 0)) * (1.0 / planes)
        y = (known[SPOT_Y : SPOT_Y + 1] + joined(known, 1)) * (1.0 / columns)
        z = (known[LAYER : LAYER + 1] + joined(known, 2)) * (1.0 / depth)
        return x, y, z

    def prepare(p):
        rows = pl.ds(pl.multiple_of(p * CHUNK, CHUNK), CHUNK)
        slot = lax.rem(p, 2)
        tile_charge_ref[slot] = mm(packed_state_ref[rows, :].astype(bf16), charge_ref[index]).astype(bf16)
        known = grouped(mm_nt(eye, packed_geo_ref[rows, :].astype(bf16)), columns)
        tile_spot_ref[slot, 0:3, :] = jnp.concatenate(places_of(known), axis=0)

    own_geo = geo_ref[0, 0, atoms : atoms + GEO, :].astype(f32)
    x, y, z = places_of(own_geo)

    def put_own(first, value):
        own_phase_ref[first : first + value.shape[0], :] = value

    phase_rows(table_ref, x, y, z, put_own)
    own_live = own_geo[LIVE : LIVE + 1].astype(bf16)
    factor_ref[...] = jnp.zeros_like(factor_ref)
    prepare(jnp.int32(0))

    def pair_step(p, carry):
        slot = lax.rem(p, 2)
        spot = tile_spot_ref[slot]
        charge = tile_charge_ref[slot]

        def put(first, value):
            phase_ref[first : first + value.shape[0], :] = value

        phase_rows(table_ref, spot[0:1], spot[1:2], spot[2:3], put)
        factor_ref[...] += mm(phase_ref[...], charge)
        prepare(jnp.minimum(p + 1, pairs - 1))
        return carry

    lax.fori_loop(0, pairs, pair_step, 0)

    full_turn = 6.283185307179586
    kx = table_ref[0] * (full_turn / planes)
    ky = table_ref[1] * (full_turn / columns)
    kz = table_ref[2] * (full_turn / depth)
    damp_ref[...] = jnp.exp(-(kx * kx + ky * ky + kz * kz) / (4.0 * screen_ref[index : index + 1, :]))
    norm = 2.0 / math.sqrt(total_atoms)
    for side in range(2):
        part = slice(side * waves, (side + 1) * waves)
        factor_ref[part, :] = factor_ref[part, :] * damp_ref[...] * norm
    damped = factor_ref[...].astype(bf16)
    field = mm_tn(own_phase_ref[...] * own_live, damped)
    field = (field * (1.0 / math.sqrt(waves))).astype(bf16)
    ewald = silu(mm(field, update_ref[index]))
    out_ref[...] = (own_ref[...].astype(f32) + ewald + conv_ref[...]).astype(bf16)


def gathered(rows, axis):
    size = lax.axis_size(axis)
    moved = [rows]
    near = [1, size - 1]
    for shift in near + list(range(2, size - 1)):
        moved.append(lax.ppermute(rows, axis, [(i, (i + shift) % size) for i in range(size)]))
    order = [0] + near + list(range(2, size - 1))
    return [moved[order.index(i)] for i in range(size)]


def shards(
    features,
    offsets,
    counts,
    wave_index,
    screening,
    charge_weight,
    ewald_weight,
    input_weight,
    filter_weight,
    middle_weight,
    output_weight,
):
    depth = counts.shape[2]
    atoms, channels = features.shape[2:]
    slots = atoms // depth
    nx = lax.axis_size("gx")
    ny = lax.axis_size("gy")
    waves = wave_index.shape[1]
    assert atoms == LANES and channels == LANES and waves % 64 == 0
    state = features.reshape(atoms, channels)
    payload = pl.pallas_call(
        pack_kernel,
        out_shape=jax.ShapeDtypeStruct((atoms + GEO, channels), bf16),
        in_specs=[smem(), vmem(), vmem()],
        out_specs=vmem(),
        name="pack",
    )(counts, features, offsets)

    rows_of = (0, 1, ny - 1)
    columns = 3 * len(rows_of)
    tall = columns + -columns % 8
    count = filter_weight.shape[1]

    def spread_out(rows):
        return gathered(jnp.stack(gathered(rows, "gy")), "gx")

    conv_call = lambda index: pl.pallas_call(
        functools.partial(conv_kernel, depth, slots, nx, ny, rows_of, index),
        out_shape=jax.ShapeDtypeStruct((atoms, channels), f32),
        in_specs=[vmem() for _ in range(10)],
        out_specs=vmem(),
        scratch_shapes=[
            pltpu.VMEM((columns * atoms, 2 * channels), bf16),
            pltpu.VMEM((depth * tall, atoms), f32),
            pltpu.VMEM((atoms, CHUNK), f32),
            pltpu.VMEM((atoms, CHUNK), f32),
            pltpu.VMEM((GROUP * count, CHUNK), bf16),
            pltpu.VMEM((count, channels), f32),
            pltpu.VMEM((count, CHUNK), f32),
            pltpu.VMEM((atoms, channels), f32),
            pltpu.VMEM((depth, CHUNK, channels), bf16),
        ],
        cost_estimate=pl.CostEstimate(flops=40_000_000_000, transcendentals=0, bytes_accessed=2_000_000),
        name="conv",
    )
    most_rows = nx * ny * atoms + 2 * CHUNK
    ewald_call = lambda block: pl.pallas_call(
        functools.partial(ewald_body if block else ewald_first, depth, nx * ny * atoms, block),
        out_shape=jax.ShapeDtypeStruct((atoms, channels), bf16),
        in_specs=[vmem() for _ in range(8 if block else 7)],
        out_specs=vmem(),
        scratch_shapes=[
            pltpu.VMEM((3, waves, LANES), f32),
            pltpu.VMEM((2 * waves, LANES), bf16),
            pltpu.VMEM((2 * waves, CHUNK), bf16),
            pltpu.VMEM((2 * waves, channels), f32),
            pltpu.VMEM((waves, channels), f32),
            pltpu.VMEM((nx, ny * atoms, LANES), bf16),
            pltpu.VMEM((nx * (ny + -ny % 8), LANES), f32),
            pltpu.VMEM((most_rows, channels), f32),
            pltpu.VMEM((most_rows, LANES), f32),
            pltpu.VMEM((2, CHUNK, channels), bf16),
            pltpu.VMEM((2, 8, CHUNK), f32),
            pltpu.SMEM((nx,), jnp.int32),
            pltpu.SMEM((nx,), jnp.int32),
        ],
        cost_estimate=pl.CostEstimate(flops=30_000_000_000, transcendentals=0, bytes_accessed=4_000_000),
        name="ewald",
    )
    geo_planes = spread_out(payload)
    geo_all = jnp.stack(geo_planes)
    state_planes, state_all = geo_planes, geo_all
    for block in range(2):
        if block:
            state_planes = spread_out(state)
            state_all = jnp.stack(state_planes)
        conv = conv_call(block)(
            geo_planes[0],
            geo_planes[1],
            geo_planes[nx - 1],
            state_planes[0],
            state_planes[1],
            state_planes[nx - 1],
            input_weight,
            filter_weight,
            middle_weight,
            output_weight,
        )
        state = ewald_call(block)(
            wave_index,
            screening,
            geo_all,
            *([state_all] if block else []),
            state,
            conv,
            charge_weight,
            ewald_weight,
        )
    return state.reshape(features.shape)


def solution(mesh):
    in_specs = (
        P("gx", "gy", None, None),
        P("gx", "gy", None, None),
        P("gx", "gy", None),
        P(),
        P(),
        P(),
        P(),
        P(),
        P(),
        P(),
        P(),
    )
    out_specs = P("gx", "gy", None, None)
    return jax.shard_map(shards, mesh=mesh, in_specs=in_specs, out_specs=out_specs, check_vma=False)
```

profile of v0, /device:TPU:29, one launch (start us, length us, event | category | flops | bytes accessed | tf_op | source)
XLA Modules:
  0.0 95.9 jit_solution(15934867740530503243)
XLA Ops:
  0.0 1.3 %copy.12.offsets_ref = f32[1,1,3,128]{3,2,1,0:T(4,128)} copy(f32[1,1,3,128]{3,1,2,0:T(1,128)} %param.12) | data formatting | bytes 3072 | tf_op args[1]
  1.3 1.4 %pack.1 = bf16[144,128]{1,0:T(8,128)(2,1)} custom-call(s32[1,1,4]{2,1,0:T(1,128)} %counts_ref.1, bf16[1,1,128,128]{3,2,1,0:T(8,128)(2,1)} %features_ref.1, f32[1,1,3,128]{3,2,1,0:T(4,128)} %copy.12.offsets_ref), custom_call_target="tpu_custom_call" | custom-call | tf_op jit(solution)/shard_map/pack/pallas_call | solution.py:488
  2.7 0.0 collective-permute-start
  2.7 1.3 %collective-permute-start.1 = (bf16[144,128]{1,0:T(8,128)(2,1)}, bf16[144,128]{1,0:T(8,128)(2,1)S(1)}, u32[]{:S(2)}, u32[]{:S(2)}) collective-permute-start(bf16[144,128]{1,0:T(8,128)(2,1)} %pack.1), channel_id=1, source_target_pairs={{0,2},{1,3},{2,0},{3,1},{4,6},{5,7},{6,4},{7,5},{8,10},{9,11},{10,... | collective-permute-start | bytes 110600 | tf_op jit(solution)/shard_map/ppermute | solution.py:462
  4.0 0.2 collective-permute-start.2
  4.2 1.5 %collective-permute-done = bf16[144,128]{1,0:T(8,128)(2,1)S(1)} collective-permute-done((bf16[144,128]{1,0:T(8,128)(2,1)}, bf16[144,128]{1,0:T(8,128)(2,1)S(1)}, u32[]{:S(2)}, u32[]{:S(2)}) %collective-permute-start) | collective-permute-done | bytes 36896 | tf_op jit(solution)/shard_map/ppermute | solution.py:462
  5.7 1.2 %collective-permute-done.1 = bf16[144,128]{1,0:T(8,128)(2,1)S(1)} collective-permute-done((bf16[144,128]{1,0:T(8,128)(2,1)}, bf16[144,128]{1,0:T(8,128)(2,1)S(1)}, u32[]{:S(2)}, u32[]{:S(2)}) %collective-permute-start.1) | collective-permute-done | bytes 36896 | tf_op jit(solution)/shard_map/ppermute | solution.py:462
  6.9 2.0 %collective-permute-done.2 = bf16[144,128]{1,0:T(8,128)(2,1)S(1)} collective-permute-done((bf16[144,128]{1,0:T(8,128)(2,1)}, bf16[144,128]{1,0:T(8,128)(2,1)S(1)}, u32[]{:S(2)}, u32[]{:S(2)}) %collective-permute-start.2) | collective-permute-done | bytes 36896 | tf_op jit(solution)/shard_map/ppermute | solution.py:462
  8.9 0.8 pad_maximum_fusion.geo_a.state_a
  9.7 3.5 %collective-permute-start.3 = (bf16[4,144,128]{2,1,0:T(8,128)(2,1)S(1)}, bf16[4,144,128]{2,1,0:T(8,128)(2,1)S(1)}, u32[]{:S(2)}, u32[]{:S(2)}) collective-permute-start(bf16[4,144,128]{2,1,0:T(8,128)(2,1)S(1)} %pad_maximum_fusion.geo_a.state_a), channel_id=1, source_target_pairs={{0,4},{4,8},{8,12},{12,16},{16,20},{20,24},{24,28},{28,0},{1,5},{5... | collective-permute-start | bytes 442376 | tf_op jit(solution)/shard_map/ppermute | solution.py:462
  13.2 0.2 collective-permute-start.4
  13.4 0.4 collective-permute-start.5
  13.7 1.2 %collective-permute-start.6 = (bf16[4,144,128]{2,1,0:T(8,128)(2,1)S(1)}, bf16[4,144,128]{2,1,0:T(8,128)(2,1)S(1)}, u32[]{:S(2)}, u32[]{:S(2)}) collective-permute-start(bf16[4,144,128]{2,1,0:T(8,128)(2,1)S(1)} %pad_maximum_fusion.geo_a.state_a), channel_id=1, source_target_pairs={{0,16},{4,20},{8,24},{12,28},{16,0},{20,4},{24,8},{28,12},{1,17},{... | collective-permute-start | bytes 442376 | tf_op jit(solution)/shard_map/ppermute | solution.py:462
  15.0 2.6 %collective-permute-start.7 = (bf16[4,144,128]{2,1,0:T(8,128)(2,1)S(1)}, bf16[4,144,128]{2,1,0:T(8,128)(2,1)S(1)}, u32[]{:S(2)}, u32[]{:S(2)}) collective-permute-start(bf16[4,144,128]{2,1,0:T(8,128)(2,1)S(1)} %pad_maximum_fusion.geo_a.state_a), channel_id=1, source_target_pairs={{0,20},{4,24},{8,28},{12,0},{16,4},{20,8},{24,12},{28,16},{1,21},{... | collective-permute-start | bytes 442376 | tf_op jit(solution)/shard_map/ppermute | solution.py:462
  17.5 0.8 bitcast_dynamic-update-slice_fusion.7
  18.3 0.0 collective-permute-done.3.geo_b.state_b
  18.3 0.3 collective-permute-start.8
  18.7 2.4 %collective-permute-done.4 = bf16[4,144,128]{2,1,0:T(8,128)(2,1)S(1)} collective-permute-done((bf16[4,144,128]{2,1,0:T(8,128)(2,1)S(1)}, bf16[4,144,128]{2,1,0:T(8,128)(2,1)S(1)}, u32[]{:S(2)}, u32[]{:S(2)}) %collective-permute-start.4) | collective-permute-done | bytes 147488 | tf_op jit(solution)/shard_map/ppermute | solution.py:462
  21.0 0.0 collective-permute-start.9
  21.1 1.9 %collective-permute-done.5 = bf16[4,144,128]{2,1,0:T(8,128)(2,1)S(1)} collective-permute-done((bf16[4,144,128]{2,1,0:T(8,128)(2,1)S(1)}, bf16[4,144,128]{2,1,0:T(8,128)(2,1)S(1)}, u32[]{:S(2)}, u32[]{:S(2)}) %collective-permute-start.5) | collective-permute-done | bytes 147488 | tf_op jit(solution)/shard_map/ppermute | solution.py:462
  23.0 4.8 %collective-permute-done.6 = bf16[4,144,128]{2,1,0:T(8,128)(2,1)S(1)} collective-permute-done((bf16[4,144,128]{2,1,0:T(8,128)(2,1)S(1)}, bf16[4,144,128]{2,1,0:T(8,128)(2,1)S(1)}, u32[]{:S(2)}, u32[]{:S(2)}) %collective-permute-start.6) | collective-permute-done | bytes 147488 | tf_op jit(solution)/shard_map/ppermute | solution.py:462
  27.8 0.1 collective-permute-done.7
  27.9 0.0 collective-permute-done.8
  28.0 0.6 copy-done.2
  28.7 14.3 %conv.2.refs_1_ = f32[128,128]{1,0:T(8,128)} custom-call(bf16[4,144,128]{2,1,0:T(8,128)(2,1)} %copy-done, bf16[4,144,128]{2,1,0:T(8,128)(2,1)} %copy-done.1, bf16[4,144,128]{2,1,0:T(8,128)(2,1)} %copy-done.2, bf16[4,144,128]{2,1,0:T(8,128)(2,1)} %copy-done, bf16[4,144,128]{2,1,0:T(8,128)(2,1)} %copy-done.1, bf16[4,144,128]{2,1,0:T(8,128)(2,1)} %copy-done.2, ...), custom_call_target="tpu_custom_call" | custom-call | flops 40000000000 | bytes 2000000 | tf_op jit(solution)/shard_map/conv/pallas_call | solution.py:554
  43.0 11.7 %ewald.2.own_ref = bf16[128,128]{1,0:T(8,128)(2,1)} custom-call(s32[3,512]{1,0:T(4,128)} %wave_ref.3, f32[2,128]{1,0:T(2,128)} %screen_ref.3, bf16[8,4,144,128]{3,2,1,0:T(8,128)(2,1)} %copy-done.7, bf16[128,128]{1,0:T(8,128)(2,1)} %bitcast.58, f32[128,128]{1,0:T(8,128)} %conv.2.refs_1_, bf16[2,128,128]{2,1,0:T(8,128)(2,1)} %charge_ref.1, ...), custom_call_target="tpu_custom_call" | custom-call | flops 30000001024 | bytes 4000000 | tf_op jit(solution)/shard_map/ewald/pallas_call | solution.py:566
  54.7 0.0 collective-permute-start.11
  54.7 1.5 %collective-permute-start.12 = (bf16[128,128]{1,0:T(8,128)(2,1)}, bf16[128,128]{1,0:T(8,128)(2,1)S(1)}, u32[]{:S(2)}, u32[]{:S(2)}) collective-permute-start(bf16[128,128]{1,0:T(8,128)(2,1)} %ewald.2.own_ref), channel_id=1, source_target_pairs={{0,3},{1,0},{2,1},{3,2},{4,7},{5,4},{6,5},{7,6},{8,11},{9,8},{10,9... | collective-permute-start | bytes 98312 | tf_op jit(solution)/shard_map/ppermute | solution.py:462
  56.1 1.5 %collective-permute-done.10 = bf16[128,128]{1,0:T(8,128)(2,1)S(1)} collective-permute-done((bf16[128,128]{1,0:T(8,128)(2,1)}, bf16[128,128]{1,0:T(8,128)(2,1)S(1)}, u32[]{:S(2)}, u32[]{:S(2)}) %collective-permute-start.10) | collective-permute-done | bytes 32800 | tf_op jit(solution)/shard_map/ppermute | solution.py:462
  57.6 0.9 collective-permute-done.11
  58.5 1.5 %collective-permute-done.12 = bf16[128,128]{1,0:T(8,128)(2,1)S(1)} collective-permute-done((bf16[128,128]{1,0:T(8,128)(2,1)}, bf16[128,128]{1,0:T(8,128)(2,1)S(1)}, u32[]{:S(2)}, u32[]{:S(2)}) %collective-permute-start.12) | collective-permute-done | bytes 32800 | tf_op jit(solution)/shard_map/ppermute | solution.py:462
  60.1 0.8 pad_maximum_fusion.1.state_a
  60.9 0.1 collective-permute-start.13
  60.9 0.5 collective-permute-start.19
  61.4 0.2 collective-permute-start.15
  61.6 2.8 %collective-permute-start.16 = (bf16[4,128,128]{2,1,0:T(8,128)(2,1)S(1)}, bf16[4,128,128]{2,1,0:T(8,128)(2,1)S(1)}, u32[]{:S(2)}, u32[]{:S(2)}) collective-permute-start(bf16[4,128,128]{2,1,0:T(8,128)(2,1)S(1)} %pad_maximum_fusion.1.state_a), channel_id=1, source_target_pairs={{0,16},{4,20},{8,24},{12,28},{16,0},{20,4},{24,8},{28,12},{1,17},{... | collective-permute-start | bytes 393224 | tf_op jit(solution)/shard_map/ppermute | solution.py:462
  64.5 0.8 bitcast_dynamic-update-slice_fusion.15
  65.2 0.0 collective-permute-done.13.state_b
  65.3 0.1 collective-permute-start.17
  65.3 0.3 collective-permute-done.19.state_c
  65.7 2.1 %collective-permute-start.18 = (bf16[4,128,128]{2,1,0:T(8,128)(2,1)S(1)}, bf16[4,128,128]{2,1,0:T(8,128)(2,1)S(1)}, u32[]{:S(2)}, u32[]{:S(2)}) collective-permute-start(bf16[4,128,128]{2,1,0:T(8,128)(2,1)S(1)} %pad_maximum_fusion.1.state_a), channel_id=1, source_target_pairs={{0,24},{4,28},{8,0},{12,4},{16,8},{20,12},{24,16},{28,20},{1,25},{... | collective-permute-start | bytes 393224 | tf_op jit(solution)/shard_map/ppermute | solution.py:462
  67.7 14.1 %conv.3.conv_ref = f32[128,128]{1,0:T(8,128)} custom-call(bf16[4,144,128]{2,1,0:T(8,128)(2,1)} %copy-done, bf16[4,144,128]{2,1,0:T(8,128)(2,1)} %copy-done.1, bf16[4,144,128]{2,1,0:T(8,128)(2,1)} %copy-done.2, bf16[4,128,128]{2,1,0:T(8,128)(2,1)} %copy-done.3, bf16[4,128,128]{2,1,0:T(8,128)(2,1)} %copy-done.6, bf16[4,128,128]{2,1,0:T(8,128)(2,1)} %copy-done.4, ...), custom_call_target="tpu_custom_call" | custom-call | flops 40000000000 | bytes 2000000 | tf_op jit(solution)/shard_map/conv/pallas_call | solution.py:554
  81.8 1.0 bitcast_dynamic-update-slice_fusion.14
  82.8 0.0 collective-permute-done.14
  82.8 0.0 collective-permute-done.16
  82.9 0.0 collective-permute-done.17
  83.0 0.9 copy-done.8
  84.0 12.0 %ewald.3 = bf16[128,128]{1,0:T(8,128)(2,1)} custom-call(s32[3,512]{1,0:T(4,128)} %wave_ref.3, f32[2,128]{1,0:T(2,128)} %screen_ref.3, bf16[8,4,144,128]{3,2,1,0:T(8,128)(2,1)} %copy-done.7, bf16[8,4,128,128]{3,2,1,0:T(8,128)(2,1)} %copy-done.8, bf16[128,128]{1,0:T(8,128)(2,1)} %ewald.2.own_ref, f32[128,128]{1,0:T(8,128)} %conv.3.conv_ref, ...), custom_call_target="tpu_custom_call" | custom-call | flops 30000001024 | bytes 4000000 | tf_op jit(solution)/shard_map/ewald/pallas_call | solution.py:566
  (34 shorter events, 0.3 us)
Async XLA Ops:
  2.7 3.0 %collective-permute-start = (bf16[144,128]{1,0:T(8,128)(2,1)}, bf16[144,128]{1,0:T(8,128)(2,1)S(1)}, u32[]{:S(2)}, u32[]{:S(2)}) collective-permute-start(bf16[144,128]{1,0:T(8,128)(2,1)} %pack.1), channel_id=1, source_target_pairs={{0,1},{1,2},{2,3},{3,0},{4,5},{5,6},{6,7},{7,4},{8,9},{9,10},{10,1... | collective-permute-start | bytes 110600 | tf_op jit(solution)/shard_map/ppermute | solution.py:462
  2.7 4.2 %collective-permute-start.1 = (bf16[144,128]{1,0:T(8,128)(2,1)}, bf16[144,128]{1,0:T(8,128)(2,1)S(1)}, u32[]{:S(2)}, u32[]{:S(2)}) collective-permute-start(bf16[144,128]{1,0:T(8,128)(2,1)} %pack.1), channel_id=1, source_target_pairs={{0,2},{1,3},{2,0},{3,1},{4,6},{5,7},{6,4},{7,5},{8,10},{9,11},{10,... | collective-permute-start | bytes 110600 | tf_op jit(solution)/shard_map/ppermute | solution.py:462
  4.0 4.9 %collective-permute-start.2 = (bf16[144,128]{1,0:T(8,128)(2,1)}, bf16[144,128]{1,0:T(8,128)(2,1)S(1)}, u32[]{:S(2)}, u32[]{:S(2)}) collective-permute-start(bf16[144,128]{1,0:T(8,128)(2,1)} %pack.1), channel_id=1, source_target_pairs={{0,3},{1,0},{2,1},{3,2},{4,7},{5,4},{6,5},{7,6},{8,11},{9,8},{10,9... | collective-permute-start | bytes 110600 | tf_op jit(solution)/shard_map/ppermute | solution.py:462
  9.7 18.4 %copy-start = (bf16[4,144,128]{2,1,0:T(8,128)(2,1)}, bf16[4,144,128]{2,1,0:T(8,128)(2,1)S(1)}, u32[]{:S(2)}) copy-start(bf16[4,144,128]{2,1,0:T(8,128)(2,1)S(1)} %pad_maximum_fusion.geo_a.state_a) | copy-start | bytes 442372
  9.7 8.6 %collective-permute-start.3 = (bf16[4,144,128]{2,1,0:T(8,128)(2,1)S(1)}, bf16[4,144,128]{2,1,0:T(8,128)(2,1)S(1)}, u32[]{:S(2)}, u32[]{:S(2)}) collective-permute-start(bf16[4,144,128]{2,1,0:T(8,128)(2,1)S(1)} %pad_maximum_fusion.geo_a.state_a), channel_id=1, source_target_pairs={{0,4},{4,8},{8,12},{12,16},{16,20},{20,24},{24,28},{28,0},{1,5},{5... | collective-permute-start | bytes 442376 | tf_op jit(solution)/shard_map/ppermute | solution.py:462
  13.2 7.9 %collective-permute-start.4 = (bf16[4,144,128]{2,1,0:T(8,128)(2,1)S(1)}, bf16[4,144,128]{2,1,0:T(8,128)(2,1)S(1)}, u32[]{:S(2)}, u32[]{:S(2)}) collective-permute-start(bf16[4,144,128]{2,1,0:T(8,128)(2,1)S(1)} %pad_maximum_fusion.geo_a.state_a), channel_id=1, source_target_pairs={{0,8},{4,12},{8,16},{12,20},{16,24},{20,28},{24,0},{28,4},{1,9},{5... | collective-permute-start | bytes 442376 | tf_op jit(solution)/shard_map/ppermute | solution.py:462
  13.4 9.6 %collective-permute-start.5 = (bf16[4,144,128]{2,1,0:T(8,128)(2,1)S(1)}, bf16[4,144,128]{2,1,0:T(8,128)(2,1)S(1)}, u32[]{:S(2)}, u32[]{:S(2)}) collective-permute-start(bf16[4,144,128]{2,1,0:T(8,128)(2,1)S(1)} %pad_maximum_fusion.geo_a.state_a), channel_id=1, source_target_pairs={{0,12},{4,16},{8,20},{12,24},{16,28},{20,0},{24,4},{28,8},{1,13},{... | collective-permute-start | bytes 442376 | tf_op jit(solution)/shard_map/ppermute | solution.py:462
  13.7 14.1 %collective-permute-start.6 = (bf16[4,144,128]{2,1,0:T(8,128)(2,1)S(1)}, bf16[4,144,128]{2,1,0:T(8,128)(2,1)S(1)}, u32[]{:S(2)}, u32[]{:S(2)}) collective-permute-start(bf16[4,144,128]{2,1,0:T(8,128)(2,1)S(1)} %pad_maximum_fusion.geo_a.state_a), channel_id=1, source_target_pairs={{0,16},{4,20},{8,24},{12,28},{16,0},{20,4},{24,8},{28,12},{1,17},{... | collective-permute-start | bytes 442376 | tf_op jit(solution)/shard_map/ppermute | solution.py:462
  15.0 12.9 %collective-permute-start.7 = (bf16[4,144,128]{2,1,0:T(8,128)(2,1)S(1)}, bf16[4,144,128]{2,1,0:T(8,128)(2,1)S(1)}, u32[]{:S(2)}, u32[]{:S(2)}) collective-permute-start(bf16[4,144,128]{2,1,0:T(8,128)(2,1)S(1)} %pad_maximum_fusion.geo_a.state_a), channel_id=1, source_target_pairs={{0,20},{4,24},{8,28},{12,0},{16,4},{20,8},{24,12},{28,16},{1,21},{... | collective-permute-start | bytes 442376 | tf_op jit(solution)/shard_map/ppermute | solution.py:462
  18.3 9.7 %copy-start.1 = (bf16[4,144,128]{2,1,0:T(8,128)(2,1)}, bf16[4,144,128]{2,1,0:T(8,128)(2,1)S(1)}, u32[]{:S(2)}) copy-start(bf16[4,144,128]{2,1,0:T(8,128)(2,1)S(1)} %collective-permute-done.3.geo_b.state_b) | copy-start | bytes 442372
  18.3 9.6 %collective-permute-start.8 = (bf16[4,144,128]{2,1,0:T(8,128)(2,1)S(1)}, bf16[4,144,128]{2,1,0:T(8,128)(2,1)S(1)}, u32[]{:S(2)}, u32[]{:S(2)}) collective-permute-start(bf16[4,144,128]{2,1,0:T(8,128)(2,1)S(1)} %pad_maximum_fusion.geo_a.state_a), channel_id=1, source_target_pairs={{0,24},{4,28},{8,0},{12,4},{16,8},{20,12},{24,16},{28,20},{1,25},{... | collective-permute-start | bytes 442376 | tf_op jit(solution)/shard_map/ppermute | solution.py:462
  21.0 6.9 %collective-permute-start.9 = (bf16[4,144,128]{2,1,0:T(8,128)(2,1)S(1)}, bf16[4,144,128]{2,1,0:T(8,128)(2,1)S(1)}, u32[]{:S(2)}, u32[]{:S(2)}) collective-permute-start(bf16[4,144,128]{2,1,0:T(8,128)(2,1)S(1)} %pad_maximum_fusion.geo_a.state_a), channel_id=1, source_target_pairs={{0,28},{4,0},{8,4},{12,8},{16,12},{20,16},{24,20},{28,24},{1,29},{... | collective-permute-start | bytes 442376 | tf_op jit(solution)/shard_map/ppermute | solution.py:462
  28.0 0.7 copy-start.2
  28.6 14.3 %copy-start.7 = (bf16[8,4,144,128]{3,2,1,0:T(8,128)(2,1)}, bf16[8,4,144,128]{3,2,1,0:T(8,128)(2,1)S(1)}, u32[]{:S(2)}) copy-start(bf16[8,4,144,128]{3,2,1,0:T(8,128)(2,1)S(1)} %bitcast_dynamic-update-slice_fusion.geo_ref) | copy-start | bytes 3538948
  54.7 3.0 %collective-permute-start.10 = (bf16[128,128]{1,0:T(8,128)(2,1)}, bf16[128,128]{1,0:T(8,128)(2,1)S(1)}, u32[]{:S(2)}, u32[]{:S(2)}) collective-permute-start(bf16[128,128]{1,0:T(8,128)(2,1)} %ewald.2.own_ref), channel_id=1, source_target_pairs={{0,1},{1,2},{2,3},{3,0},{4,5},{5,6},{6,7},{7,4},{8,9},{9,10},{10,1... | collective-permute-start | bytes 98312 | tf_op jit(solution)/shard_map/ppermute | solution.py:462
  54.7 3.9 %collective-permute-start.11 = (bf16[128,128]{1,0:T(8,128)(2,1)}, bf16[128,128]{1,0:T(8,128)(2,1)S(1)}, u32[]{:S(2)}, u32[]{:S(2)}) collective-permute-start(bf16[128,128]{1,0:T(8,128)(2,1)} %ewald.2.own_ref), channel_id=1, source_target_pairs={{0,2},{1,3},{2,0},{3,1},{4,6},{5,7},{6,4},{7,5},{8,10},{9,11},{10,... | collective-permute-start | bytes 98312 | tf_op jit(solution)/shard_map/ppermute | solution.py:462
  54.7 5.4 %collective-permute-start.12 = (bf16[128,128]{1,0:T(8,128)(2,1)}, bf16[128,128]{1,0:T(8,128)(2,1)S(1)}, u32[]{:S(2)}, u32[]{:S(2)}) collective-permute-start(bf16[128,128]{1,0:T(8,128)(2,1)} %ewald.2.own_ref), channel_id=1, source_target_pairs={{0,3},{1,0},{2,1},{3,2},{4,7},{5,4},{6,5},{7,6},{8,11},{9,8},{10,9... | collective-permute-start | bytes 98312 | tf_op jit(solution)/shard_map/ppermute | solution.py:462
  60.8 6.9 %copy-start.3 = (bf16[4,128,128]{2,1,0:T(8,128)(2,1)}, bf16[4,128,128]{2,1,0:T(8,128)(2,1)S(1)}, u32[]{:S(2)}) copy-start(bf16[4,128,128]{2,1,0:T(8,128)(2,1)S(1)} %pad_maximum_fusion.1.state_a) | copy-start | bytes 393220
  60.9 4.4 %collective-permute-start.13 = (bf16[4,128,128]{2,1,0:T(8,128)(2,1)S(1)}, bf16[4,128,128]{2,1,0:T(8,128)(2,1)S(1)}, u32[]{:S(2)}, u32[]{:S(2)}) collective-permute-start(bf16[4,128,128]{2,1,0:T(8,128)(2,1)S(1)} %pad_maximum_fusion.1.state_a), channel_id=1, source_target_pairs={{0,4},{4,8},{8,12},{12,16},{16,20},{20,24},{24,28},{28,0},{1,5},{5... | collective-permute-start | bytes 393224 | tf_op jit(solution)/shard_map/ppermute | solution.py:462
  60.9 4.7 %collective-permute-start.19 = (bf16[4,128,128]{2,1,0:T(8,128)(2,1)S(1)}, bf16[4,128,128]{2,1,0:T(8,128)(2,1)S(1)}, u32[]{:S(2)}, u32[]{:S(2)}) collective-permute-start(bf16[4,128,128]{2,1,0:T(8,128)(2,1)S(1)} %pad_maximum_fusion.1.state_a), channel_id=1, source_target_pairs={{0,28},{4,0},{8,4},{12,8},{16,12},{20,16},{24,20},{28,24},{1,29},{... | collective-permute-start | bytes 393224 | tf_op jit(solution)/shard_map/ppermute | solution.py:462
  61.4 21.4 %collective-permute-start.14 = (bf16[4,128,128]{2,1,0:T(8,128)(2,1)S(1)}, bf16[4,128,128]{2,1,0:T(8,128)(2,1)S(1)}, u32[]{:S(2)}, u32[]{:S(2)}) collective-permute-start(bf16[4,128,128]{2,1,0:T(8,128)(2,1)S(1)} %pad_maximum_fusion.1.state_a), channel_id=1, source_target_pairs={{0,8},{4,12},{8,16},{12,20},{16,24},{20,28},{24,0},{28,4},{1,9},{5... | collective-permute-start | bytes 393224 | tf_op jit(solution)/shard_map/ppermute | solution.py:462
  61.4 21.4 %collective-permute-start.15 = (bf16[4,128,128]{2,1,0:T(8,128)(2,1)S(1)}, bf16[4,128,128]{2,1,0:T(8,128)(2,1)S(1)}, u32[]{:S(2)}, u32[]{:S(2)}) collective-permute-start(bf16[4,128,128]{2,1,0:T(8,128)(2,1)S(1)} %pad_maximum_fusion.1.state_a), channel_id=1, source_target_pairs={{0,12},{4,16},{8,20},{12,24},{16,28},{20,0},{24,4},{28,8},{1,13},{... | collective-permute-start | bytes 393224 | tf_op jit(solution)/shard_map/ppermute | solution.py:462
  61.6 21.2 %collective-permute-start.16 = (bf16[4,128,128]{2,1,0:T(8,128)(2,1)S(1)}, bf16[4,128,128]{2,1,0:T(8,128)(2,1)S(1)}, u32[]{:S(2)}, u32[]{:S(2)}) collective-permute-start(bf16[4,128,128]{2,1,0:T(8,128)(2,1)S(1)} %pad_maximum_fusion.1.state_a), channel_id=1, source_target_pairs={{0,16},{4,20},{8,24},{12,28},{16,0},{20,4},{24,8},{28,12},{1,17},{... | collective-permute-start | bytes 393224 | tf_op jit(solution)/shard_map/ppermute | solution.py:462
  65.2 2.5 %copy-start.6 = (bf16[4,128,128]{2,1,0:T(8,128)(2,1)}, bf16[4,128,128]{2,1,0:T(8,128)(2,1)S(1)}, u32[]{:S(2)}) copy-start(bf16[4,128,128]{2,1,0:T(8,128)(2,1)S(1)} %collective-permute-done.13.state_b) | copy-start | bytes 393220
  65.3 17.6 %collective-permute-start.17 = (bf16[4,128,128]{2,1,0:T(8,128)(2,1)S(1)}, bf16[4,128,128]{2,1,0:T(8,128)(2,1)S(1)}, u32[]{:S(2)}, u32[]{:S(2)}) collective-permute-start(bf16[4,128,128]{2,1,0:T(8,128)(2,1)S(1)} %pad_maximum_fusion.1.state_a), channel_id=1, source_target_pairs={{0,20},{4,24},{8,28},{12,0},{16,4},{20,8},{24,12},{28,16},{1,21},{... | collective-permute-start | bytes 393224 | tf_op jit(solution)/shard_map/ppermute | solution.py:462
  65.7 2.1 %copy-start.4 = (bf16[4,128,128]{2,1,0:T(8,128)(2,1)}, bf16[4,128,128]{2,1,0:T(8,128)(2,1)S(1)}, u32[]{:S(2)}) copy-start(bf16[4,128,128]{2,1,0:T(8,128)(2,1)S(1)} %collective-permute-done.19.state_c) | copy-start | bytes 393220
  65.7 17.3 %collective-permute-start.18 = (bf16[4,128,128]{2,1,0:T(8,128)(2,1)S(1)}, bf16[4,128,128]{2,1,0:T(8,128)(2,1)S(1)}, u32[]{:S(2)}, u32[]{:S(2)}) collective-permute-start(bf16[4,128,128]{2,1,0:T(8,128)(2,1)S(1)} %pad_maximum_fusion.1.state_a), channel_id=1, source_target_pairs={{0,24},{4,28},{8,0},{12,4},{16,8},{20,12},{24,16},{28,20},{1,25},{... | collective-permute-start | bytes 393224 | tf_op jit(solution)/shard_map/ppermute | solution.py:462
  81.8 1.2 %copy-start.5 = (bf16[4,128,128]{2,1,0:T(8,128)(2,1)S(1)}, bf16[4,128,128]{2,1,0:T(8,128)(2,1)}, u32[]{:S(2)}) copy-start(bf16[4,128,128]{2,1,0:T(8,128)(2,1)} %copy-done.4) | copy-start | bytes 393220
  83.0 1.0 copy-start.8
where the time goes:
time: 96.6 us; the launch traced here: 95.9 us
  Pallas kernels  53.5 us (55%)
  waiting for transfers between devices  18.2 us (19%)
  starting transfers between devices  16.9 us (17%)
  local copies, waits for them, and re-layouts  4.07 us (4%)
  other arithmetic  3.11 us (3%)
    pallas_call x2, Pallas kernels, shards(): conv_call(block)  28.4 us
    pallas_call x2, Pallas kernels, shards(): ewald_call(block)  23.7 us
    ppermute x20, waiting for transfers between devices, gathered(): lax.ppermute(rows, axis, [(i, (i + shift) % size) for i in range(size)])  18.2 us
    ppermute x20, starting transfers between devices, gathered(): lax.ppermute(rows, axis, [(i, (i + shift) % size) for i in range(size)])  16.9 us
    unnamed x31, local copies, waits for them, and re-layouts  4.02 us
  transfers between devices with their start and end apart: 20, of which 11 were waited for; matrix products, arithmetic and copies ran while one was open for 3% of the time, Pallas kernels for 15%

commit v1 on v0

--- a/solution.py
+++ b/solution.py
@@ -13,9 +13,8 @@
 bf16 = jnp.bfloat16
 
 LANES = 128
-PARTS = 3
 GEO = 16
-LIVE, SPOT_X, SPOT_Y, LAYER, SLOT = 9, 10, 11, 12, 13
+LIVE, LOW, SLOT, MID, SPOT = 3, 4, 7, 8, 11
 CHUNK = 256
 GROUP = 16
 NONE = -1.0e30
@@ -88,23 +87,19 @@
     atoms, _ = features_ref.shape[2:]
     slots = atoms // depth
     out_ref[0:atoms, :] = features_ref[0, 0]
-    rows = []
-    for axis in range(3):
-        rest = offsets_ref[0, 0, axis : axis + 1, :]
-        for _ in range(PARTS):
-            piece = rest.astype(bf16).astype(f32)
-            rows.append(piece)
-            rest = rest - piece
     lane = iota((1, atoms), 1)
     limit = jnp.zeros((1, atoms), jnp.int32)
     for cell in range(depth):
         limit = jnp.where(lane // slots == cell, counts_ref[0, 0, cell], limit)
-    rows.append((lane - (lane // slots) * slots < limit).astype(f32))
+    offset = offsets_ref[...]
+    high = offset.astype(bf16).astype(f32)
+    middle = (offset - high).astype(bf16).astype(f32)
+    low = (offset - high) - middle
+    rows = [high, (lane - (lane // slots) * slots < limit).astype(f32), low, (lane + 1).astype(f32), middle]
     rows.append(jnp.full((1, atoms), lax.axis_index("gx"), jnp.int32).astype(f32))
     rows.append(jnp.full((1, atoms), lax.axis_index("gy"), jnp.int32).astype(f32))
     rows.append((lane // slots).astype(f32))
-    rows.append((lane + 1).astype(f32))
-    rows.append(jnp.zeros((GEO - len(rows), atoms), f32))
+    rows.append(jnp.zeros((2, atoms), f32))
     out_ref[atoms : atoms + GEO, :] = jnp.concatenate(rows, axis=0).astype(bf16)
 
 
@@ -132,8 +127,8 @@
 
 
 def joined(known, axis):
-    parts = [known[PARTS * axis + p : PARTS * axis + p + 1] for p in range(PARTS)]
-    return (parts[0] + parts[1]) + parts[2]
+    high, middle, low = [known[axis + r : axis + r + 1] for r in (0, MID, LOW)]
+    return (high + middle) + low
 
 
 def grouped(known, groups):
@@ -192,25 +187,25 @@
     spots = [[], [], [], [], [], []]
     for plane in range(3):
         known = jnp.concatenate([geo[plane][row, atoms : atoms + GEO, :] for row in rows_of], axis=0)
-        turned = mm_nt(eye, known)
+        fill = jnp.zeros((channels - near * GEO, atoms), bf16)
+        turned = mm_nt(eye, jnp.concatenate([known, fill], axis=0))
         group = iota(turned.shape, 1) // GEO
         wide = known.astype(f32)
         if plane == 0:
-            here_x = wide[SPOT_X : SPOT_X + 1, 0:1]
-            here_y = wide[SPOT_Y : SPOT_Y + 1, 0:1]
+            here_x = wide[SPOT : SPOT + 1, 0:1]
+            here_y = wide[SPOT + 1 : SPOT + 2, 0:1]
             target = [
-                (turned[:, PARTS * a : PARTS * a + 1] + turned[:, PARTS * a + 1 : PARTS * a + 2])
-                + turned[:, PARTS * a + 2 : PARTS * a + 3]
+                (turned[:, a : a + 1] + turned[:, MID + a : MID + a + 1]) + turned[:, LOW + a : LOW + a + 1]
                 for a in range(3)
             ]
         for i, row in enumerate(rows_of):
             part = slice((plane * near + i) * atoms, (plane * near + i + 1) * atoms)
             source_ref[part, 0:channels] = mm(state[plane][row, 0:atoms, :], input_ref[index]).astype(bf16)
-            source_ref[part, channels : channels + near * GEO] = jnp.where(group == i, turned, 0.0).astype(bf16)
+            source_ref[part, channels : 2 * channels] = jnp.where(group == i, turned, 0.0).astype(bf16)
             own = wide[i * GEO : (i + 1) * GEO]
             for a in range(3):
                 spots[a].append(joined(own, a))
-            for a, r in ((3, LIVE), (4, SPOT_X), (5, SPOT_Y)):
+            for a, r in ((3, LIVE), (4, SPOT), (5, SPOT + 1)):
                 spots[a].append(own[r : r + 1])
     fill = [jnp.zeros((block - columns, atoms), f32)]
     x, y, z, live, at_x, at_y = [jnp.concatenate(rows + fill, axis=0) for rows in spots]
@@ -240,9 +235,9 @@
             mapped_ref[cell, 0:width, :] = found[:, 0:channels].astype(bf16)
             known = grouped(mm_nt(pick_rows, found[:, channels : 2 * channels].astype(bf16)), near)
             part = slice(cell * slots, (cell + 1) * slots)
-            along_x = wrapped(known[SPOT_X : SPOT_X + 1] - here_x, size_x)
-            along_y = wrapped(known[SPOT_Y : SPOT_Y + 1] - here_y, size_y)
-            along_z = wrapped(known[LAYER : LAYER + 1] - float(cell), depth)
+            along_x = wrapped(known[SPOT : SPOT + 1] - here_x, size_x)
+            along_y = wrapped(known[SPOT + 1 : SPOT + 2] - here_y, size_y)
+            along_z = wrapped(known[SPOT + 2 : SPOT + 3] - float(cell), depth)
             home = jnp.abs(along_x) + jnp.abs(along_y)
             who = jnp.where(home == 0.0, known[SLOT : SLOT + 1], 0.0)
             diff_x = (along_x + joined(known, 0)) - target[0][part, :]
@@ -307,151 +302,187 @@
         put(waves + first, (power_sum(SIN_TURN, square) * rest).astype(bf16))
 
 
-def ewald_first(depth, total_atoms, index, wave_ref, screen_ref, geo_ref, *refs):
-    ewald_body(depth, total_atoms, index, wave_ref, screen_ref, geo_ref, geo_ref, *refs)
-
-
-def ewald_body(
-    depth,
-    total_atoms,
-    index,
-    wave_ref,
-    screen_ref,
-    geo_ref,
-    state_ref,
-    own_ref,
-    conv_ref,
-    charge_ref,
-    update_ref,
-    out_ref,
-    table_ref,
-    own_phase_ref,
-    phase_ref,
-    factor_ref,
-    damp_ref,
-    turned_ref,
-    place_ref,
-    packed_state_ref,
-    packed_geo_ref,
-    tile_charge_ref,
-    tile_spot_ref,
-    first_ref,
-    number_ref,
-):
-    planes, columns = geo_ref.shape[0], geo_ref.shape[1]
-    atoms, channels = own_ref.shape
+def wave_columns(wave_ref, table_ref):
     waves = wave_ref.shape[1]
-    eye = identity(atoms, atoms)
+    eye = identity(LANES, LANES)
     numbers = jnp.concatenate([wave_ref[...].astype(f32), jnp.zeros((5, waves), f32)], axis=0).astype(bf16)
     for first in range(0, waves, LANES):
         turned = mm_nt(eye, numbers[:, first : first + LANES])
         for a in range(3):
             table_ref[a, first : first + LANES, :] = jnp.broadcast_to(turned[:, a : a + 1], (LANES, LANES))
-    block = columns + -columns % 8
-
-    def plane_live(s, carry):
-        lives = [geo_ref[s, t, atoms + LIVE : atoms + LIVE + 1, :].astype(f32) for t in range(columns)]
-        if block > columns:
-            lives.append(jnp.zeros((block - columns, atoms), f32))
-        live = jnp.concatenate(lives, axis=0)
-        place_ref[pl.ds(pl.multiple_of(s * block, block), block), :] = live
-        known = jnp.concatenate([geo_ref[s, t, atoms : atoms + GEO, :] for t in range(columns)], axis=0)
-        if columns * GEO < LANES:
-            known = jnp.concatenate([known, jnp.zeros((LANES - columns * GEO, atoms), bf16)], axis=0)
-        turned = mm_nt(eye, known)
-        group = iota(turned.shape, 1) // GEO
-        for t in range(columns):
-            turned_ref[s, t * atoms : (t + 1) * atoms, :] = jnp.where(group == t, turned, 0.0).astype(bf16)
-        number = jnp.sum(live).astype(jnp.int32)
-        number_ref[s] = number
-        first_ref[s] = carry[0]
-        return carry[0] + number, jnp.maximum(carry[1], number)
-
-    unroll = 8 if planes % 8 == 0 else 1
-    total, most = lax.fori_loop(0, planes, plane_live, (jnp.int32(0), jnp.int32(0)), unroll=unroll)
-    place_ref[...] = places(place_ref[...], block)
-    pairs = (total + (CHUNK - 1)) // CHUNK
-
-    def clear(p, carry):
-        packed_state_ref[pl.ds(pl.multiple_of(p * LANES, LANES), LANES), :] = jnp.zeros((LANES, channels), f32)
-        packed_geo_ref[pl.ds(pl.multiple_of(p * LANES, LANES), LANES), :] = jnp.zeros((LANES, LANES), f32)
-        return carry
-
-    lax.fori_loop(0, 2 * pairs + 2, clear, 0)
-
-    def pick_step(j, carry):
-        def plane_step(s, carry):
-            start = pl.multiple_of(s * block, block)
-            place = place_ref[pl.ds(start, block), :][0:columns]
-            want = chosen(place, j * LANES, LANES)
-            picked = mm(want, state_ref[s, :, 0:atoms, :].reshape(columns * atoms, channels))
-            spots = mm(want, turned_ref[s])
-
-            @pl.when(j * LANES < number_ref[s])
-            def _():
-                rows = pl.ds(first_ref[s] + j * LANES, LANES)
-                packed_state_ref[rows, :] += picked
-                packed_geo_ref[rows, :] += spots
-
+
+
+def ewald_kernel(
+    depth,
+    total_atoms,
+    index,
+    keep,
+    reuse,
+    *refs,
+):
+    refs = list(refs)
+    if reuse:
+        base_ref = refs.pop(0)
+        own_phase_ref, kept_ref = refs.pop(0), refs.pop(0)
+        wave_ref, screen_ref, state_ref, own_ref, conv_ref, charge_ref, update_ref, out_ref = refs[:8]
+        refs = refs[8:]
+        planes, columns = state_ref.shape[0], state_ref.shape[1]
+    else:
+        wave_ref, screen_ref, geo_ref = refs[:3]
+        refs = refs[3:]
+        state_ref = geo_ref if index == 0 else refs.pop(0)
+        own_ref, conv_ref, charge_ref, update_ref, out_ref = refs[:5]
+        refs = refs[5:]
+        if keep:
+            base_out_ref, own_phase_ref, kept_ref = refs[:3]
+            refs = refs[3:]
+        else:
+            own_phase_ref, base_out_ref = refs[:2]
+            refs = refs[2:]
+        base_ref, rows_ref, turned_ref, live_ref, packed_geo_ref, spot_ref, base_sem = refs[:7]
+        refs = refs[7:]
+        planes, columns = geo_ref.shape[0], geo_ref.shape[1]
+    table_ref, phase_ref, factor_ref, damp_ref, packed_ref, tile_ref, phase_sem = refs
+    atoms, channels = own_ref.shape
+    slots = atoms // depth
+    waves = wave_ref.shape[1]
+    everyone = planes * columns
+    wave_columns(wave_ref, table_ref)
+
+    if not reuse:
+        row = iota((3, 1), 0)
+        unit = jnp.where(row == 0, 1.0 / planes, jnp.where(row == 1, 1.0 / columns, 1.0 / depth))
+
+        def plane_rows(s, carry):
+            spots, lives = [], []
+            for t in range(columns):
+                known = geo_ref[s, t, atoms : atoms + GEO, :].astype(f32)
+                offset = (known[0:3] + known[MID : MID + 3]) + known[LOW : LOW + 3]
+                spots += [(known[SPOT : SPOT + 3] + offset) * unit, jnp.zeros((1, atoms), f32)]
+                lives.append(known[LIVE : LIVE + 1])
+            tall = 4 * columns
+            rows_ref[pl.ds(pl.multiple_of(s * tall, tall), tall), :] = jnp.concatenate(spots, axis=0)
+            live_ref[pl.ds(pl.multiple_of(s * columns, columns), columns), :] = jnp.concatenate(lives, axis=0)
             return carry
 
-        return lax.fori_loop(0, planes, plane_step, carry, unroll=unroll)
-
-    lax.fori_loop(0, (most + (LANES - 1)) // LANES, pick_step, 0)
-
-    def places_of(known):
-        x = (known[SPOT_X : SPOT_X + 1] + joined(known, 0)) * (1.0 / planes)
-        y = (known[SPOT_Y : SPOT_Y + 1] + joined(known, 1)) * (1.0 / columns)
-        z = (known[LAYER : LAYER + 1] + joined(known, 2)) * (1.0 / depth)
-        return x, y, z
-
-    def prepare(p):
-        rows = pl.ds(pl.multiple_of(p * CHUNK, CHUNK), CHUNK)
-        slot = lax.rem(p, 2)
-        tile_charge_ref[slot] = mm(packed_state_ref[rows, :].astype(bf16), charge_ref[index]).astype(bf16)
-        known = grouped(mm_nt(eye, packed_geo_ref[rows, :].astype(bf16)), columns)
-        tile_spot_ref[slot, 0:3, :] = jnp.concatenate(places_of(known), axis=0)
-
-    own_geo = geo_ref[0, 0, atoms : atoms + GEO, :].astype(f32)
-    x, y, z = places_of(own_geo)
-
-    def put_own(first, value):
-        own_phase_ref[first : first + value.shape[0], :] = value
-
-    phase_rows(table_ref, x, y, z, put_own)
-    own_live = own_geo[LIVE : LIVE + 1].astype(bf16)
-    factor_ref[...] = jnp.zeros_like(factor_ref)
-    prepare(jnp.int32(0))
-
-    def pair_step(p, carry):
-        slot = lax.rem(p, 2)
-        spot = tile_spot_ref[slot]
-        charge = tile_charge_ref[slot]
-
-        def put(first, value):
-            phase_ref[first : first + value.shape[0], :] = value
-
-        phase_rows(table_ref, spot[0:1], spot[1:2], spot[2:3], put)
-        factor_ref[...] += mm(phase_ref[...], charge)
-        prepare(jnp.minimum(p + 1, pairs - 1))
-        return carry
-
-    lax.fori_loop(0, pairs, pair_step, 0)
+        lax.fori_loop(0, planes, plane_rows, 0, unroll=4 if planes % 4 == 0 else 1)
+        live = live_ref[...]
+        before = (iota((atoms, atoms), 0) < iota((atoms, atoms), 1)).astype(f32).astype(bf16)
+        live_b = live.astype(bf16)
+        number = mm(live_b, jnp.ones((atoms, atoms), bf16))
+        above = (iota((everyone, everyone), 1) < iota((everyone, everyone), 0)).astype(f32).astype(bf16)
+        start = mm(above, number.astype(bf16))
+        base_out_ref[0:everyone, :] = (mm(live_b, before) + start).astype(jnp.int32)
+        last = (number + start)[everyone - 1 : everyone, :].astype(jnp.int32)
+        base_out_ref[everyone : everyone + 8, :] = jnp.broadcast_to(last, (8, atoms))
+        base_copy = pltpu.make_async_copy(base_out_ref, base_ref, base_sem)
+        base_copy.start()
+        for b in range(turned_ref.shape[0]):
+            turned_ref[b] = rows_ref[b * LANES : (b + 1) * LANES, :].T
+        own_rows = geo_ref[0, 0, atoms : atoms + GEO, :].astype(f32)
+        offset = (own_rows[0:3] + own_rows[MID : MID + 3]) + own_rows[LOW : LOW + 3]
+        own_spot = (own_rows[SPOT : SPOT + 3] + offset) * unit
+        own_live = own_rows[LIVE : LIVE + 1].astype(bf16)
+
+        def put_own(first, value):
+            own_phase_ref[first : first + value.shape[0], :] = value * own_live
+
+        phase_rows(table_ref, own_spot[0:1], own_spot[1:2], own_spot[2:3], put_own)
 
     full_turn = 6.283185307179586
     kx = table_ref[0] * (full_turn / planes)
     ky = table_ref[1] * (full_turn / columns)
     kz = table_ref[2] * (full_turn / depth)
-    damp_ref[...] = jnp.exp(-(kx * kx + ky * ky + kz * kz) / (4.0 * screen_ref[index : index + 1, :]))
     norm = 2.0 / math.sqrt(total_atoms)
+    damp_ref[...] = norm * jnp.exp(-(kx * kx + ky * ky + kz * kz) / (4.0 * screen_ref[index : index + 1, :]))
+    factor_ref[...] = jnp.zeros_like(factor_ref)
+    if not reuse:
+        base_copy.wait()
+    total = base_ref[everyone, 0]
+    pairs = (total + (CHUNK - 1)) // CHUNK
+
+    def phase_copy(p, slot):
+        if reuse:
+            return pltpu.make_async_copy(kept_ref.at[p], phase_ref.at[slot], phase_sem.at[slot])
+        return pltpu.make_async_copy(phase_ref.at[slot], kept_ref.at[p], phase_sem.at[slot])
+
+    if reuse:
+        phase_copy(0, 0).start()
+
+    def pack_step(s, carry):
+        for t in range(columns):
+            c = s * columns + t
+            for cell in range(depth):
+                rows = pl.ds(base_ref[c, cell * slots], slots)
+                part = slice(cell * slots, (cell + 1) * slots)
+                packed_ref[rows, :] = state_ref[s, t, part, :].astype(f32)
+                if not reuse:
+                    spread = LANES // 4
+                    mine = iota((slots, LANES), 1) // 4 == lax.rem(c, spread)
+                    packed_geo_ref[rows, :] = jnp.where(mine, turned_ref[c // spread, part, :], 0.0)
+        return carry
+
+    lax.fori_loop(0, planes, pack_step, 0, unroll=2 if planes % 2 == 0 else 1)
+
+    def prepare(p):
+        rows = pl.ds(pl.multiple_of(p * CHUNK, CHUNK), CHUNK)
+        slot = lax.rem(p, 2)
+        valid = iota((CHUNK, channels), 0) + p * CHUNK < total
+        picked = jnp.where(valid, packed_ref[rows, :], 0.0).astype(bf16)
+        tile_ref[slot] = mm(picked, charge_ref[index]).astype(bf16)
+        if not reuse:
+            known = packed_geo_ref[rows, :].T
+            known = jnp.sum(known.reshape(LANES // 8, 8, CHUNK), axis=0)
+            known = known[0:4] + known[4:8]
+            valid = iota((4, CHUNK), 1) + p * CHUNK < total
+            spot_ref[slot, 0:4, :] = jnp.where(valid, known, 0.0)
+
+    prepare(jnp.int32(0))
+
+    def pair_step(p, carry):
+        slot = lax.rem(p, 2)
+        charge = tile_ref[slot]
+        if reuse:
+
+            @pl.when(p + 1 < pairs)
+            def _():
+                phase_copy(p + 1, 1 - slot).start()
+
+            phase_copy(p, slot).wait()
+        else:
+            spot = spot_ref[slot]
+            if keep:
+
+                @pl.when(p >= 2)
+                def _():
+                    phase_copy(p - 2, slot).wait()
+
+            def put(first, value):
+                phase_ref[slot, first : first + value.shape[0], :] = value
+
+            phase_rows(table_ref, spot[0:1], spot[1:2], spot[2:3], put)
+        factor_ref[...] += mm(phase_ref[slot], charge)
+        if keep and not reuse:
+            phase_copy(p, slot).start()
+        prepare(jnp.minimum(p + 1, pairs - 1))
+        return carry
+
+    lax.fori_loop(0, pairs, pair_step, 0)
     for side in range(2):
         part = slice(side * waves, (side + 1) * waves)
-        factor_ref[part, :] = factor_ref[part, :] * damp_ref[...] * norm
+        factor_ref[part, :] = factor_ref[part, :] * damp_ref[...]
     damped = factor_ref[...].astype(bf16)
-    field = mm_tn(own_phase_ref[...] * own_live, damped)
+    field = mm_tn(own_phase_ref[...], damped)
     field = (field * (1.0 / math.sqrt(waves))).astype(bf16)
     ewald = silu(mm(field, update_ref[index]))
     out_ref[...] = (own_ref[...].astype(f32) + ewald + conv_ref[...]).astype(bf16)
+    if keep and not reuse:
+
+        @pl.when(pairs >= 2)
+        def _():
+            phase_copy(pairs - 2, lax.rem(pairs, 2)).wait()
+
+        phase_copy(pairs - 1, lax.rem(pairs + 1, 2)).wait()
 
 
 def gathered(rows, axis):
@@ -491,7 +522,7 @@
         in_specs=[smem(), vmem(), vmem()],
         out_specs=vmem(),
         name="pack",
-    )(counts, features, offsets)
+    )(counts, features, offsets.reshape(3, atoms))
 
     rows_of = (0, 1, ny - 1)
     columns = 3 * len(rows_of)
@@ -520,30 +551,54 @@
         cost_estimate=pl.CostEstimate(flops=40_000_000_000, transcendentals=0, bytes_accessed=2_000_000),
         name="conv",
     )
-    most_rows = nx * ny * atoms + 2 * CHUNK
-    ewald_call = lambda block: pl.pallas_call(
-        functools.partial(ewald_body if block else ewald_first, depth, nx * ny * atoms, block),
-        out_shape=jax.ShapeDtypeStruct((atoms, channels), bf16),
-        in_specs=[vmem() for _ in range(8 if block else 7)],
-        out_specs=vmem(),
-        scratch_shapes=[
-            pltpu.VMEM((3, waves, LANES), f32),
-            pltpu.VMEM((2 * waves, LANES), bf16),
-            pltpu.VMEM((2 * waves, CHUNK), bf16),
-            pltpu.VMEM((2 * waves, channels), f32),
-            pltpu.VMEM((waves, channels), f32),
-            pltpu.VMEM((nx, ny * atoms, LANES), bf16),
-            pltpu.VMEM((nx * (ny + -ny % 8), LANES), f32),
-            pltpu.VMEM((most_rows, channels), f32),
+    everyone = nx * ny
+    most_pairs = -(-everyone * atoms // CHUNK)
+    keep = most_pairs * 2 * waves * CHUNK * 2 <= 16 * 2**20
+    most_rows = most_pairs * CHUNK + slots
+
+    def ewald_call(index, *operands):
+        reuse = keep and index > 0
+        geometry = [] if reuse else [
+            pltpu.SMEM((everyone + 8, atoms), jnp.int32),
+            pltpu.VMEM((everyone * 4, LANES), f32),
+            pltpu.VMEM((everyone * 4 // LANES, LANES, LANES), f32),
+            pltpu.VMEM((everyone, atoms), f32),
             pltpu.VMEM((most_rows, LANES), f32),
-            pltpu.VMEM((2, CHUNK, channels), bf16),
             pltpu.VMEM((2, 8, CHUNK), f32),
-            pltpu.SMEM((nx,), jnp.int32),
-            pltpu.SMEM((nx,), jnp.int32),
-        ],
-        cost_estimate=pl.CostEstimate(flops=30_000_000_000, transcendentals=0, bytes_accessed=4_000_000),
-        name="ewald",
-    )
+            pltpu.SemaphoreType.DMA,
+        ]
+        own_phase, base = ((2 * waves, LANES), bf16), ((everyone + 8, atoms), jnp.int32)
+        out_shape = [jax.ShapeDtypeStruct((atoms, channels), bf16)]
+        out_specs = [vmem()]
+        in_specs = [vmem() for _ in operands]
+        hbm = pl.BlockSpec(memory_space=pl.ANY)
+        if reuse:
+            in_specs[0], in_specs[2] = smem(), hbm
+        elif keep:
+            out_shape += [jax.ShapeDtypeStruct(*base[:2]), jax.ShapeDtypeStruct(*own_phase[:2])]
+            out_shape.append(jax.ShapeDtypeStruct((most_pairs, 2 * waves, CHUNK), bf16))
+            out_specs += [vmem(), vmem(), hbm]
+        else:
+            geometry = [pltpu.VMEM(*own_phase), pltpu.VMEM(*base)] + geometry
+        return pl.pallas_call(
+            functools.partial(ewald_kernel, depth, everyone * atoms, index, keep, reuse),
+            out_shape=out_shape,
+            in_specs=in_specs,
+            out_specs=out_specs,
+            scratch_shapes=geometry
+            + [
+                pltpu.VMEM((3, waves, LANES), f32),
+                pltpu.VMEM((2, 2 * waves, CHUNK), bf16),
+                pltpu.VMEM((2 * waves, channels), f32),
+                pltpu.VMEM((waves, channels), f32),
+                pltpu.VMEM((most_rows, channels), f32),
+                pltpu.VMEM((2, CHUNK, channels), bf16),
+                pltpu.SemaphoreType.DMA((2,)),
+            ],
+            cost_estimate=pl.CostEstimate(flops=30_000_000_000, transcendentals=0, bytes_accessed=4_000_000),
+            name="ewald",
+        )(*operands)
+
     geo_planes = spread_out(payload)
     geo_all = jnp.stack(geo_planes)
     state_planes, state_all = geo_planes, geo_all
@@ -563,16 +618,13 @@
             middle_weight,
             output_weight,
         )
-        state = ewald_call(block)(
-            wave_index,
-            screening,
-            geo_all,
-            *([state_all] if block else []),
-            state,
-            conv,
-            charge_weight,
-            ewald_weight,
-        )
+        common = (state, conv, charge_weight, ewald_weight)
+        if block == 0:
+            state, *kept = ewald_call(block, wave_index, screening, geo_all, *common)
+        elif keep:
+            (state,) = ewald_call(block, *kept, wave_index, screening, state_all, *common)
+        else:
+            (state,) = ewald_call(block, wave_index, screening, geo_all, state_all, *common)
     return state.reshape(features.shape)
 
 

time: 96.6 us -> 87 us (0.901)
  Pallas kernels: 53.5 us -> 43.7 us
    pallas_call x2, Pallas kernels: 23.7 us -> 14.1 us  [ewald_call(): pl.pallas_call(functools.partial(ewald_kernel, depth, everyone * atoms, i...]
  transfers between devices with their start and end apart: 20 -> 20, of which waited for: 11 -> 11; matrix products, arithmetic and copies ran while one was open for 3% -> 3% of each run, Pallas kernels for 15% -> 16%
where the time goes in v1:
time: 87 us; the launch traced here: 86.3 us
  Pallas kernels  43.7 us (50%)
  waiting for transfers between devices  18.2 us (21%)
  starting transfers between devices  16.9 us (19%)
  local copies, waits for them, and re-layouts  4.16 us (5%)
  other arithmetic  3.12 us (4%)
    pallas_call x2, Pallas kernels, shards(): conv_call(block)  28.2 us
    ppermute x20, waiting for transfers between devices, gathered(): lax.ppermute(rows, axis, [(i, (i + shift) % size) for i in range(size)])  18.2 us
    ppermute x20, starting transfers between devices, gathered(): lax.ppermute(rows, axis, [(i, (i + shift) % size) for i in range(size)])  16.9 us
    pallas_call x2, Pallas kernels, ewald_call(): pl.pallas_call(functools.partial(ewald_kernel, depth, everyone * atoms, i...  14.1 us
    unnamed x31, local copies, waits for them, and re-layouts  4.12 us
  transfers between devices with their start and end apart: 20, of which 11 were waited for; matrix products, arithmetic and copies ran while one was open for 3% of the time, Pallas kernels for 16%

profile of v1, /device:TPU:29, one launch (start us, length us, event | category | flops | bytes accessed | tf_op | source)
XLA Modules:
  0.0 86.3 jit_solution(9897689655168135388)
XLA Ops:
  0.0 1.3 %copy.14 = f32[1,1,3,128]{3,2,1,0:T(4,128)} copy(f32[1,1,3,128]{3,1,2,0:T(1,128)} %param.12) | data formatting | bytes 3072
  1.3 1.4 %pack.1 = bf16[144,128]{1,0:T(8,128)(2,1)} custom-call(s32[1,1,4]{2,1,0:T(1,128)} %counts_ref.1, bf16[1,1,128,128]{3,2,1,0:T(8,128)(2,1)} %features_ref.1, f32[3,128]{1,0:T(4,128)} %bitcast.62), custom_call_target="tpu_custom_call" | custom-call | tf_op jit(solution)/shard_map/pack/pallas_call | solution.py:519
  2.7 0.0 collective-permute-start
  2.7 1.3 %collective-permute-start.1 = (bf16[144,128]{1,0:T(8,128)(2,1)}, bf16[144,128]{1,0:T(8,128)(2,1)S(1)}, u32[]{:S(2)}, u32[]{:S(2)}) collective-permute-start(bf16[144,128]{1,0:T(8,128)(2,1)} %pack.1), channel_id=1, source_target_pairs={{0,2},{1,3},{2,0},{3,1},{4,6},{5,7},{6,4},{7,5},{8,10},{9,11},{10,... | collective-permute-start | bytes 110600 | tf_op jit(solution)/shard_map/ppermute | solution.py:493
  4.0 0.2 collective-permute-start.2
  4.2 1.5 %collective-permute-done = bf16[144,128]{1,0:T(8,128)(2,1)S(1)} collective-permute-done((bf16[144,128]{1,0:T(8,128)(2,1)}, bf16[144,128]{1,0:T(8,128)(2,1)S(1)}, u32[]{:S(2)}, u32[]{:S(2)}) %collective-permute-start) | collective-permute-done | bytes 36896 | tf_op jit(solution)/shard_map/ppermute | solution.py:493
  5.7 1.2 %collective-permute-done.1 = bf16[144,128]{1,0:T(8,128)(2,1)S(1)} collective-permute-done((bf16[144,128]{1,0:T(8,128)(2,1)}, bf16[144,128]{1,0:T(8,128)(2,1)S(1)}, u32[]{:S(2)}, u32[]{:S(2)}) %collective-permute-start.1) | collective-permute-done | bytes 36896 | tf_op jit(solution)/shard_map/ppermute | solution.py:493
  6.9 2.0 %collective-permute-done.2 = bf16[144,128]{1,0:T(8,128)(2,1)S(1)} collective-permute-done((bf16[144,128]{1,0:T(8,128)(2,1)}, bf16[144,128]{1,0:T(8,128)(2,1)S(1)}, u32[]{:S(2)}, u32[]{:S(2)}) %collective-permute-start.2) | collective-permute-done | bytes 36896 | tf_op jit(solution)/shard_map/ppermute | solution.py:493
  8.9 0.8 pad_maximum_fusion.geo_a.state_a
  9.7 3.5 %collective-permute-start.3 = (bf16[4,144,128]{2,1,0:T(8,128)(2,1)S(1)}, bf16[4,144,128]{2,1,0:T(8,128)(2,1)S(1)}, u32[]{:S(2)}, u32[]{:S(2)}) collective-permute-start(bf16[4,144,128]{2,1,0:T(8,128)(2,1)S(1)} %pad_maximum_fusion.geo_a.state_a), channel_id=1, source_target_pairs={{0,4},{4,8},{8,12},{12,16},{16,20},{20,24},{24,28},{28,0},{1,5},{5... | collective-permute-start | bytes 442376 | tf_op jit(solution)/shard_map/ppermute | solution.py:493
  13.2 0.2 collective-permute-start.4
  13.4 0.4 collective-permute-start.5
  13.7 1.2 %collective-permute-start.6 = (bf16[4,144,128]{2,1,0:T(8,128)(2,1)S(1)}, bf16[4,144,128]{2,1,0:T(8,128)(2,1)S(1)}, u32[]{:S(2)}, u32[]{:S(2)}) collective-permute-start(bf16[4,144,128]{2,1,0:T(8,128)(2,1)S(1)} %pad_maximum_fusion.geo_a.state_a), channel_id=1, source_target_pairs={{0,16},{4,20},{8,24},{12,28},{16,0},{20,4},{24,8},{28,12},{1,17},{... | collective-permute-start | bytes 442376 | tf_op jit(solution)/shard_map/ppermute | solution.py:493
  15.0 2.6 %collective-permute-start.7 = (bf16[4,144,128]{2,1,0:T(8,128)(2,1)S(1)}, bf16[4,144,128]{2,1,0:T(8,128)(2,1)S(1)}, u32[]{:S(2)}, u32[]{:S(2)}) collective-permute-start(bf16[4,144,128]{2,1,0:T(8,128)(2,1)S(1)} %pad_maximum_fusion.geo_a.state_a), channel_id=1, source_target_pairs={{0,20},{4,24},{8,28},{12,0},{16,4},{20,8},{24,12},{28,16},{1,21},{... | collective-permute-start | bytes 442376 | tf_op jit(solution)/shard_map/ppermute | solution.py:493
  17.5 0.8 bitcast_dynamic-update-slice_fusion.7
  18.3 0.3 collective-permute-start.8
  18.7 2.4 %collective-permute-done.4 = bf16[4,144,128]{2,1,0:T(8,128)(2,1)S(1)} collective-permute-done((bf16[4,144,128]{2,1,0:T(8,128)(2,1)S(1)}, bf16[4,144,128]{2,1,0:T(8,128)(2,1)S(1)}, u32[]{:S(2)}, u32[]{:S(2)}) %collective-permute-start.4) | collective-permute-done | bytes 147488 | tf_op jit(solution)/shard_map/ppermute | solution.py:493
  21.1 1.9 %collective-permute-done.5 = bf16[4,144,128]{2,1,0:T(8,128)(2,1)S(1)} collective-permute-done((bf16[4,144,128]{2,1,0:T(8,128)(2,1)S(1)}, bf16[4,144,128]{2,1,0:T(8,128)(2,1)S(1)}, u32[]{:S(2)}, u32[]{:S(2)}) %collective-permute-start.5) | collective-permute-done | bytes 147488 | tf_op jit(solution)/shard_map/ppermute | solution.py:493
  23.0 4.8 %collective-permute-done.6 = bf16[4,144,128]{2,1,0:T(8,128)(2,1)S(1)} collective-permute-done((bf16[4,144,128]{2,1,0:T(8,128)(2,1)S(1)}, bf16[4,144,128]{2,1,0:T(8,128)(2,1)S(1)}, u32[]{:S(2)}, u32[]{:S(2)}) %collective-permute-start.6) | collective-permute-done | bytes 147488 | tf_op jit(solution)/shard_map/ppermute | solution.py:493
  27.8 0.1 collective-permute-done.7
  27.9 0.0 collective-permute-done.8
  28.0 0.0 collective-permute-done.9.geo_c.state_c
  28.0 0.6 copy-done.2
  28.6 14.3 %conv.2.refs_4_ = f32[128,128]{1,0:T(8,128)} custom-call(bf16[4,144,128]{2,1,0:T(8,128)(2,1)} %copy-done, bf16[4,144,128]{2,1,0:T(8,128)(2,1)} %copy-done.1, bf16[4,144,128]{2,1,0:T(8,128)(2,1)} %copy-done.2, bf16[4,144,128]{2,1,0:T(8,128)(2,1)} %copy-done, bf16[4,144,128]{2,1,0:T(8,128)(2,1)} %copy-done.1, bf16[4,144,128]{2,1,0:T(8,128)(2,1)} %copy-done.2, ...), custom_call_target="tpu_custom_call" | custom-call | flops 40000000000 | bytes 2000000 | tf_op jit(solution)/shard_map/conv/pallas_call | solution.py:609
  43.0 8.1 %ewald.2 = (bf16[128,128]{1,0:T(8,128)(2,1)}, s32[40,128]{1,0:T(8,128)}, bf16[1024,128]{1,0:T(8,128)(2,1)}, bf16[16,1024,256]{2,1,0:T(8,128)(2,1)}) custom-call(s32[3,512]{1,0:T(4,128)} %refs_3_.1, f32[2,128]{1,0:T(2,128)} %refs_4_.1, bf16[8,4,144,128]{3,2,1,0:T(8,128)(2,1)} %copy-done.7, bf16[128,128]{1,0:T(8,128)(2,1)} %bitcast.61, ...), custom_call_target="tpu_custom_call" | custom-call | flops 30000001024 | bytes 4000000 | tf_op jit(solution)/shard_map/ewald/pallas_call | solution.py:583
  51.1 0.1 collective-permute-start.10
  51.2 0.1 collective-permute-start.11
  51.2 1.4 %collective-permute-start.12 = (bf16[128,128]{1,0:T(8,128)(2,1)}, bf16[128,128]{1,0:T(8,128)(2,1)S(1)}, u32[]{:S(2)}, u32[]{:S(2)}) collective-permute-start(bf16[128,128]{1,0:T(8,128)(2,1)} %get-tuple-element.12.refs_6_), channel_id=1, source_target_pairs={{0,3},{1,0},{2,1},{3,2},{4,7},{5,4},{6,5},{7,6},{8,11},{9,8},{10,9... | collective-permute-start | bytes 98312 | tf_op jit(solution)/shard_map/ppermute | solution.py:493
  52.6 1.5 %collective-permute-done.10 = bf16[128,128]{1,0:T(8,128)(2,1)S(1)} collective-permute-done((bf16[128,128]{1,0:T(8,128)(2,1)}, bf16[128,128]{1,0:T(8,128)(2,1)S(1)}, u32[]{:S(2)}, u32[]{:S(2)}) %collective-permute-start.10) | collective-permute-done | bytes 32800 | tf_op jit(solution)/shard_map/ppermute | solution.py:493
  54.1 1.0 %collective-permute-done.11 = bf16[128,128]{1,0:T(8,128)(2,1)S(1)} collective-permute-done((bf16[128,128]{1,0:T(8,128)(2,1)}, bf16[128,128]{1,0:T(8,128)(2,1)S(1)}, u32[]{:S(2)}, u32[]{:S(2)}) %collective-permute-start.11) | collective-permute-done | bytes 32800 | tf_op jit(solution)/shard_map/ppermute | solution.py:493
  55.1 1.5 %collective-permute-done.12 = bf16[128,128]{1,0:T(8,128)(2,1)S(1)} collective-permute-done((bf16[128,128]{1,0:T(8,128)(2,1)}, bf16[128,128]{1,0:T(8,128)(2,1)S(1)}, u32[]{:S(2)}, u32[]{:S(2)}) %collective-permute-start.12) | collective-permute-done | bytes 32800 | tf_op jit(solution)/shard_map/ppermute | solution.py:493
  56.5 0.8 pad_maximum_fusion.1.state_a
  57.3 0.1 collective-permute-start.13
  57.4 0.5 collective-permute-start.19
  57.9 0.0 collective-permute-start.14
  57.9 0.2 collective-permute-start.15
  58.1 2.8 %collective-permute-start.16 = (bf16[4,128,128]{2,1,0:T(8,128)(2,1)S(1)}, bf16[4,128,128]{2,1,0:T(8,128)(2,1)S(1)}, u32[]{:S(2)}, u32[]{:S(2)}) collective-permute-start(bf16[4,128,128]{2,1,0:T(8,128)(2,1)S(1)} %pad_maximum_fusion.1.state_a), channel_id=1, source_target_pairs={{0,16},{4,20},{8,24},{12,28},{16,0},{20,4},{24,8},{28,12},{1,17},{... | collective-permute-start | bytes 393224 | tf_op jit(solution)/shard_map/ppermute | solution.py:493
  61.0 0.8 bitcast_dynamic-update-slice_fusion.15
  61.7 0.0 collective-permute-done.13.state_b
  61.7 0.1 collective-permute-start.17
  61.8 0.3 collective-permute-done.19.state_c
  62.1 2.1 %collective-permute-start.18 = (bf16[4,128,128]{2,1,0:T(8,128)(2,1)S(1)}, bf16[4,128,128]{2,1,0:T(8,128)(2,1)S(1)}, u32[]{:S(2)}, u32[]{:S(2)}) collective-permute-start(bf16[4,128,128]{2,1,0:T(8,128)(2,1)S(1)} %pad_maximum_fusion.1.state_a), channel_id=1, source_target_pairs={{0,24},{4,28},{8,0},{12,4},{16,8},{20,12},{24,16},{28,20},{1,25},{... | collective-permute-start | bytes 393224 | tf_op jit(solution)/shard_map/ppermute | solution.py:493
  64.2 13.9 %conv.3.refs_7_ = f32[128,128]{1,0:T(8,128)} custom-call(bf16[4,144,128]{2,1,0:T(8,128)(2,1)} %copy-done, bf16[4,144,128]{2,1,0:T(8,128)(2,1)} %copy-done.1, bf16[4,144,128]{2,1,0:T(8,128)(2,1)} %copy-done.2, bf16[4,128,128]{2,1,0:T(8,128)(2,1)} %copy-done.3, bf16[4,128,128]{2,1,0:T(8,128)(2,1)} %copy-done.6, bf16[4,128,128]{2,1,0:T(8,128)(2,1)} %copy-done.4, ...), custom_call_target="tpu_custom_call" | custom-call | flops 40000000000 | bytes 2000000 | tf_op jit(solution)/shard_map/conv/pallas_call | solution.py:609
  78.1 1.0 %bitcast_dynamic-update-slice_fusion.14 = bf16[8,4,128,128]{3,2,1,0:T(8,128)(2,1)S(1)} fusion(bf16[8,4,128,128]{3,2,1,0:T(8,128)(2,1)S(1)} %bitcast_dynamic-update-slice_fusion.15, bf16[4,128,128]{2,1,0:T(8,128)(2,1)} %copy-done.6), kind=kLoop, calls=%fused_computation.16 | loop fusion | bytes 262144
  79.2 0.0 collective-permute-done.16
  79.2 0.0 collective-permute-done.17
  79.3 1.0 %copy-done.8 = bf16[8,4,128,128]{3,2,1,0:T(8,128)(2,1)} copy-done((bf16[8,4,128,128]{3,2,1,0:T(8,128)(2,1)}, bf16[8,4,128,128]{3,2,1,0:T(8,128)(2,1)S(1)}, u32[]{:S(2)}) %copy-start.8) | copy-done | bytes 1048600
  80.4 6.0 %ewald.3 = bf16[128,128]{1,0:T(8,128)(2,1)} custom-call(s32[40,128]{1,0:T(8,128)} %get-tuple-element.9.refs_0_, bf16[1024,128]{1,0:T(8,128)(2,1)} %get-tuple-element.10.refs_1_, bf16[16,1024,256]{2,1,0:T(8,128)(2,1)} %get-tuple-element.11.refs_2_, s32[3,512]{1,0:T(4,128)} %refs_3_.1, f32[2,128]{1,0:T(2,128)} %refs_4_.1, bf16[8,4,128,128]{3,2,1,0:T(8,128)(2,1)} %copy-done.8, ...), custom_call_target="tpu_custom_call" | custom-call | flops 30000001024 | bytes 4000000 | tf_op jit(solution)/shard_map/ewald/pallas_call | solution.py:583
  (34 shorter events, 0.3 us)
Async XLA Ops:
  2.7 3.0 %collective-permute-start = (bf16[144,128]{1,0:T(8,128)(2,1)}, bf16[144,128]{1,0:T(8,128)(2,1)S(1)}, u32[]{:S(2)}, u32[]{:S(2)}) collective-permute-start(bf16[144,128]{1,0:T(8,128)(2,1)} %pack.1), channel_id=1, source_target_pairs={{0,1},{1,2},{2,3},{3,0},{4,5},{5,6},{6,7},{7,4},{8,9},{9,10},{10,1... | collective-permute-start | bytes 110600 | tf_op jit(solution)/shard_map/ppermute | solution.py:493
  2.7 4.2 %collective-permute-start.1 = (bf16[144,128]{1,0:T(8,128)(2,1)}, bf16[144,128]{1,0:T(8,128)(2,1)S(1)}, u32[]{:S(2)}, u32[]{:S(2)}) collective-permute-start(bf16[144,128]{1,0:T(8,128)(2,1)} %pack.1), channel_id=1, source_target_pairs={{0,2},{1,3},{2,0},{3,1},{4,6},{5,7},{6,4},{7,5},{8,10},{9,11},{10,... | collective-permute-start | bytes 110600 | tf_op jit(solution)/shard_map/ppermute | solution.py:493
  4.0 4.9 %collective-permute-start.2 = (bf16[144,128]{1,0:T(8,128)(2,1)}, bf16[144,128]{1,0:T(8,128)(2,1)S(1)}, u32[]{:S(2)}, u32[]{:S(2)}) collective-permute-start(bf16[144,128]{1,0:T(8,128)(2,1)} %pack.1), channel_id=1, source_target_pairs={{0,3},{1,0},{2,1},{3,2},{4,7},{5,4},{6,5},{7,6},{8,11},{9,8},{10,9... | collective-permute-start | bytes 110600 | tf_op jit(solution)/shard_map/ppermute | solution.py:493
  9.7 18.4 %copy-start = (bf16[4,144,128]{2,1,0:T(8,128)(2,1)}, bf16[4,144,128]{2,1,0:T(8,128)(2,1)S(1)}, u32[]{:S(2)}) copy-start(bf16[4,144,128]{2,1,0:T(8,128)(2,1)S(1)} %pad_maximum_fusion.geo_a.state_a) | copy-start | bytes 442372
  9.7 8.6 %collective-permute-start.3 = (bf16[4,144,128]{2,1,0:T(8,128)(2,1)S(1)}, bf16[4,144,128]{2,1,0:T(8,128)(2,1)S(1)}, u32[]{:S(2)}, u32[]{:S(2)}) collective-permute-start(bf16[4,144,128]{2,1,0:T(8,128)(2,1)S(1)} %pad_maximum_fusion.geo_a.state_a), channel_id=1, source_target_pairs={{0,4},{4,8},{8,12},{12,16},{16,20},{20,24},{24,28},{28,0},{1,5},{5... | collective-permute-start | bytes 442376 | tf_op jit(solution)/shard_map/ppermute | solution.py:493
  13.2 7.9 %collective-permute-start.4 = (bf16[4,144,128]{2,1,0:T(8,128)(2,1)S(1)}, bf16[4,144,128]{2,1,0:T(8,128)(2,1)S(1)}, u32[]{:S(2)}, u32[]{:S(2)}) collective-permute-start(bf16[4,144,128]{2,1,0:T(8,128)(2,1)S(1)} %pad_maximum_fusion.geo_a.state_a), channel_id=1, source_target_pairs={{0,8},{4,12},{8,16},{12,20},{16,24},{20,28},{24,0},{28,4},{1,9},{5... | collective-permute-start | bytes 442376 | tf_op jit(solution)/shard_map/ppermute | solution.py:493
  13.4 9.6 %collective-permute-start.5 = (bf16[4,144,128]{2,1,0:T(8,128)(2,1)S(1)}, bf16[4,144,128]{2,1,0:T(8,128)(2,1)S(1)}, u32[]{:S(2)}, u32[]{:S(2)}) collective-permute-start(bf16[4,144,128]{2,1,0:T(8,128)(2,1)S(1)} %pad_maximum_fusion.geo_a.state_a), channel_id=1, source_target_pairs={{0,12},{4,16},{8,20},{12,24},{16,28},{20,0},{24,4},{28,8},{1,13},{... | collective-permute-start | bytes 442376 | tf_op jit(solution)/shard_map/ppermute | solution.py:493
  13.7 14.1 %collective-permute-start.6 = (bf16[4,144,128]{2,1,0:T(8,128)(2,1)S(1)}, bf16[4,144,128]{2,1,0:T(8,128)(2,1)S(1)}, u32[]{:S(2)}, u32[]{:S(2)}) collective-permute-start(bf16[4,144,128]{2,1,0:T(8,128)(2,1)S(1)} %pad_maximum_fusion.geo_a.state_a), channel_id=1, source_target_pairs={{0,16},{4,20},{8,24},{12,28},{16,0},{20,4},{24,8},{28,12},{1,17},{... | collective-permute-start | bytes 442376 | tf_op jit(solution)/shard_map/ppermute | solution.py:493
  15.0 12.9 %collective-permute-start.7 = (bf16[4,144,128]{2,1,0:T(8,128)(2,1)S(1)}, bf16[4,144,128]{2,1,0:T(8,128)(2,1)S(1)}, u32[]{:S(2)}, u32[]{:S(2)}) collective-permute-start(bf16[4,144,128]{2,1,0:T(8,128)(2,1)S(1)} %pad_maximum_fusion.geo_a.state_a), channel_id=1, source_target_pairs={{0,20},{4,24},{8,28},{12,0},{16,4},{20,8},{24,12},{28,16},{1,21},{... | collective-permute-start | bytes 442376 | tf_op jit(solution)/shard_map/ppermute | solution.py:493
  18.3 9.7 %copy-start.1 = (bf16[4,144,128]{2,1,0:T(8,128)(2,1)}, bf16[4,144,128]{2,1,0:T(8,128)(2,1)S(1)}, u32[]{:S(2)}) copy-start(bf16[4,144,128]{2,1,0:T(8,128)(2,1)S(1)} %collective-permute-done.3.geo_b.state_b) | copy-start | bytes 442372
  18.3 9.6 %collective-permute-start.8 = (bf16[4,144,128]{2,1,0:T(8,128)(2,1)S(1)}, bf16[4,144,128]{2,1,0:T(8,128)(2,1)S(1)}, u32[]{:S(2)}, u32[]{:S(2)}) collective-permute-start(bf16[4,144,128]{2,1,0:T(8,128)(2,1)S(1)} %pad_maximum_fusion.geo_a.state_a), channel_id=1, source_target_pairs={{0,24},{4,28},{8,0},{12,4},{16,8},{20,12},{24,16},{28,20},{1,25},{... | collective-permute-start | bytes 442376 | tf_op jit(solution)/shard_map/ppermute | solution.py:493
  21.0 6.9 %collective-permute-start.9 = (bf16[4,144,128]{2,1,0:T(8,128)(2,1)S(1)}, bf16[4,144,128]{2,1,0:T(8,128)(2,1)S(1)}, u32[]{:S(2)}, u32[]{:S(2)}) collective-permute-start(bf16[4,144,128]{2,1,0:T(8,128)(2,1)S(1)} %pad_maximum_fusion.geo_a.state_a), channel_id=1, source_target_pairs={{0,28},{4,0},{8,4},{12,8},{16,12},{20,16},{24,20},{28,24},{1,29},{... | collective-permute-start | bytes 442376 | tf_op jit(solution)/shard_map/ppermute | solution.py:493
  28.0 0.7 copy-start.2
  28.6 14.3 %copy-start.7 = (bf16[8,4,144,128]{3,2,1,0:T(8,128)(2,1)}, bf16[8,4,144,128]{3,2,1,0:T(8,128)(2,1)S(1)}, u32[]{:S(2)}) copy-start(bf16[8,4,144,128]{3,2,1,0:T(8,128)(2,1)S(1)} %bitcast_dynamic-update-slice_fusion.refs_2_) | copy-start | bytes 3538948
  51.1 3.0 %collective-permute-start.10 = (bf16[128,128]{1,0:T(8,128)(2,1)}, bf16[128,128]{1,0:T(8,128)(2,1)S(1)}, u32[]{:S(2)}, u32[]{:S(2)}) collective-permute-start(bf16[128,128]{1,0:T(8,128)(2,1)} %get-tuple-element.12.refs_6_), channel_id=1, source_target_pairs={{0,1},{1,2},{2,3},{3,0},{4,5},{5,6},{6,7},{7,4},{8,9},{9,10},{10,1... | collective-permute-start | bytes 98312 | tf_op jit(solution)/shard_map/ppermute | solution.py:493
  51.2 3.9 %collective-permute-start.11 = (bf16[128,128]{1,0:T(8,128)(2,1)}, bf16[128,128]{1,0:T(8,128)(2,1)S(1)}, u32[]{:S(2)}, u32[]{:S(2)}) collective-permute-start(bf16[128,128]{1,0:T(8,128)(2,1)} %get-tuple-element.12.refs_6_), channel_id=1, source_target_pairs={{0,2},{1,3},{2,0},{3,1},{4,6},{5,7},{6,4},{7,5},{8,10},{9,11},{10,... | collective-permute-start | bytes 98312 | tf_op jit(solution)/shard_map/ppermute | solution.py:493
  51.2 5.3 %collective-permute-start.12 = (bf16[128,128]{1,0:T(8,128)(2,1)}, bf16[128,128]{1,0:T(8,128)(2,1)S(1)}, u32[]{:S(2)}, u32[]{:S(2)}) collective-permute-start(bf16[128,128]{1,0:T(8,128)(2,1)} %get-tuple-element.12.refs_6_), channel_id=1, source_target_pairs={{0,3},{1,0},{2,1},{3,2},{4,7},{5,4},{6,5},{7,6},{8,11},{9,8},{10,9... | collective-permute-start | bytes 98312 | tf_op jit(solution)/shard_map/ppermute | solution.py:493
  57.3 6.9 %copy-start.3 = (bf16[4,128,128]{2,1,0:T(8,128)(2,1)}, bf16[4,128,128]{2,1,0:T(8,128)(2,1)S(1)}, u32[]{:S(2)}) copy-start(bf16[4,128,128]{2,1,0:T(8,128)(2,1)S(1)} %pad_maximum_fusion.1.state_a) | copy-start | bytes 393220
  57.3 4.4 %collective-permute-start.13 = (bf16[4,128,128]{2,1,0:T(8,128)(2,1)S(1)}, bf16[4,128,128]{2,1,0:T(8,128)(2,1)S(1)}, u32[]{:S(2)}, u32[]{:S(2)}) collective-permute-start(bf16[4,128,128]{2,1,0:T(8,128)(2,1)S(1)} %pad_maximum_fusion.1.state_a), channel_id=1, source_target_pairs={{0,4},{4,8},{8,12},{12,16},{16,20},{20,24},{24,28},{28,0},{1,5},{5... | collective-permute-start | bytes 393224 | tf_op jit(solution)/shard_map/ppermute | solution.py:493
  57.4 4.7 %collective-permute-start.19 = (bf16[4,128,128]{2,1,0:T(8,128)(2,1)S(1)}, bf16[4,128,128]{2,1,0:T(8,128)(2,1)S(1)}, u32[]{:S(2)}, u32[]{:S(2)}) collective-permute-start(bf16[4,128,128]{2,1,0:T(8,128)(2,1)S(1)} %pad_maximum_fusion.1.state_a), channel_id=1, source_target_pairs={{0,28},{4,0},{8,4},{12,8},{16,12},{20,16},{24,20},{28,24},{1,29},{... | collective-permute-start | bytes 393224 | tf_op jit(solution)/shard_map/ppermute | solution.py:493
  57.9 21.2 %collective-permute-start.14 = (bf16[4,128,128]{2,1,0:T(8,128)(2,1)S(1)}, bf16[4,128,128]{2,1,0:T(8,128)(2,1)S(1)}, u32[]{:S(2)}, u32[]{:S(2)}) collective-permute-start(bf16[4,128,128]{2,1,0:T(8,128)(2,1)S(1)} %pad_maximum_fusion.1.state_a), channel_id=1, source_target_pairs={{0,8},{4,12},{8,16},{12,20},{16,24},{20,28},{24,0},{28,4},{1,9},{5... | collective-permute-start | bytes 393224 | tf_op jit(solution)/shard_map/ppermute | solution.py:493
  57.9 21.2 %collective-permute-start.15 = (bf16[4,128,128]{2,1,0:T(8,128)(2,1)S(1)}, bf16[4,128,128]{2,1,0:T(8,128)(2,1)S(1)}, u32[]{:S(2)}, u32[]{:S(2)}) collective-permute-start(bf16[4,128,128]{2,1,0:T(8,128)(2,1)S(1)} %pad_maximum_fusion.1.state_a), channel_id=1, source_target_pairs={{0,12},{4,16},{8,20},{12,24},{16,28},{20,0},{24,4},{28,8},{1,13},{... | collective-permute-start | bytes 393224 | tf_op jit(solution)/shard_map/ppermute | solution.py:493
  58.1 21.0 %collective-permute-start.16 = (bf16[4,128,128]{2,1,0:T(8,128)(2,1)S(1)}, bf16[4,128,128]{2,1,0:T(8,128)(2,1)S(1)}, u32[]{:S(2)}, u32[]{:S(2)}) collective-permute-start(bf16[4,128,128]{2,1,0:T(8,128)(2,1)S(1)} %pad_maximum_fusion.1.state_a), channel_id=1, source_target_pairs={{0,16},{4,20},{8,24},{12,28},{16,0},{20,4},{24,8},{28,12},{1,17},{... | collective-permute-start | bytes 393224 | tf_op jit(solution)/shard_map/ppermute | solution.py:493
  61.7 2.5 %copy-start.6 = (bf16[4,128,128]{2,1,0:T(8,128)(2,1)}, bf16[4,128,128]{2,1,0:T(8,128)(2,1)S(1)}, u32[]{:S(2)}) copy-start(bf16[4,128,128]{2,1,0:T(8,128)(2,1)S(1)} %collective-permute-done.13.state_b) | copy-start | bytes 393220
  61.7 17.5 %collective-permute-start.17 = (bf16[4,128,128]{2,1,0:T(8,128)(2,1)S(1)}, bf16[4,128,128]{2,1,0:T(8,128)(2,1)S(1)}, u32[]{:S(2)}, u32[]{:S(2)}) collective-permute-start(bf16[4,128,128]{2,1,0:T(8,128)(2,1)S(1)} %pad_maximum_fusion.1.state_a), channel_id=1, source_target_pairs={{0,20},{4,24},{8,28},{12,0},{16,4},{20,8},{24,12},{28,16},{1,21},{... | collective-permute-start | bytes 393224 | tf_op jit(solution)/shard_map/ppermute | solution.py:493
  62.1 2.1 %copy-start.4 = (bf16[4,128,128]{2,1,0:T(8,128)(2,1)}, bf16[4,128,128]{2,1,0:T(8,128)(2,1)S(1)}, u32[]{:S(2)}) copy-start(bf16[4,128,128]{2,1,0:T(8,128)(2,1)S(1)} %collective-permute-done.19.state_c) | copy-start | bytes 393220
  62.1 17.1 %collective-permute-start.18 = (bf16[4,128,128]{2,1,0:T(8,128)(2,1)S(1)}, bf16[4,128,128]{2,1,0:T(8,128)(2,1)S(1)}, u32[]{:S(2)}, u32[]{:S(2)}) collective-permute-start(bf16[4,128,128]{2,1,0:T(8,128)(2,1)S(1)} %pad_maximum_fusion.1.state_a), channel_id=1, source_target_pairs={{0,24},{4,28},{8,0},{12,4},{16,8},{20,12},{24,16},{28,20},{1,25},{... | collective-permute-start | bytes 393224 | tf_op jit(solution)/shard_map/ppermute | solution.py:493
  78.1 1.2 %copy-start.5 = (bf16[4,128,128]{2,1,0:T(8,128)(2,1)S(1)}, bf16[4,128,128]{2,1,0:T(8,128)(2,1)}, u32[]{:S(2)}) copy-start(bf16[4,128,128]{2,1,0:T(8,128)(2,1)} %copy-done.4) | copy-start | bytes 393220
  79.3 1.1 %copy-start.8 = (bf16[8,4,128,128]{3,2,1,0:T(8,128)(2,1)}, bf16[8,4,128,128]{3,2,1,0:T(8,128)(2,1)S(1)}, u32[]{:S(2)}) copy-start(bf16[8,4,128,128]{3,2,1,0:T(8,128)(2,1)S(1)} %bitcast_dynamic-update-slice_fusion.8.refs_5_) | copy-start | bytes 3145732

commit v2 on v1

--- a/solution.py
+++ b/solution.py
@@ -18,6 +18,8 @@
 CHUNK = 256
 GROUP = 16
 NONE = -1.0e30
+INPUT, FILTER, MIDDLE, OUTPUT = range(4)
+AHEAD = 5
 
 COS_TURN = (
     1.0,
@@ -160,10 +162,7 @@
     state_a,
     state_b,
     state_c,
-    input_ref,
-    filter_ref,
-    middle_ref,
-    output_ref,
+    weight_all_ref,
     out_ref,
     source_ref,
     place_ref,
@@ -176,7 +175,8 @@
     mapped_ref,
 ):
     atoms, channels = message_ref.shape
-    count = filter_ref.shape[1]
+    count = weight_all_ref.shape[1]
+    input_at, filter_at, middle_at, output_at = [2 * kind + index for kind in (INPUT, FILTER, MIDDLE, OUTPUT)]
     spread = math.sqrt(0.25 * math.log2(math.e))
     geo = (geo_a, geo_b, geo_c)
     state = (state_a, state_b, state_c)
@@ -200,7 +200,7 @@
             ]
         for i, row in enumerate(rows_of):
             part = slice((plane * near + i) * atoms, (plane * near + i + 1) * atoms)
-            source_ref[part, 0:channels] = mm(state[plane][row, 0:atoms, :], input_ref[index]).astype(bf16)
+            source_ref[part, 0:channels] = mm(state[plane][row, 0:atoms, :], weight_all_ref[input_at]).astype(bf16)
             source_ref[part, channels : 2 * channels] = jnp.where(group == i, turned, 0.0).astype(bf16)
             own = wide[i * GEO : (i + 1) * GEO]
             for a in range(3):
@@ -224,7 +224,7 @@
         longest = jnp.maximum(longest, totals[-1])
     place_ref[...] = places(jnp.concatenate(lives, axis=0), block)
     center_ref[...] = iota((count, CHUNK), 0).astype(f32) * spread
-    wide_ref[...] = filter_ref[index].astype(f32)
+    wide_ref[...] = weight_all_ref[filter_at].astype(f32)
     message_ref[...] = jnp.zeros_like(message_ref)
     pick_rows = identity(near * GEO, atoms)
 
@@ -283,8 +283,8 @@
     def _():
         piece(full * CHUNK, LANES)
 
-    middle = silu(mm(message_ref[...].astype(bf16), middle_ref[index])).astype(bf16)
-    out_ref[...] = mm(middle, output_ref[index])
+    middle = silu(mm(message_ref[...].astype(bf16), weight_all_ref[middle_at])).astype(bf16)
+    out_ref[...] = mm(middle, weight_all_ref[output_at])
 
 
 def phase_rows(wave_ref, x, y, z, put):
@@ -407,7 +407,11 @@
         return pltpu.make_async_copy(phase_ref.at[slot], kept_ref.at[p], phase_sem.at[slot])
 
     if reuse:
-        phase_copy(0, 0).start()
+        for p in range(AHEAD - 1):
+
+            @pl.when(p < pairs)
+            def _(p=p):
+                phase_copy(p, p).start()
 
     def pack_step(s, carry):
         for t in range(columns):
@@ -444,12 +448,15 @@
         charge = tile_ref[slot]
         if reuse:
 
-            @pl.when(p + 1 < pairs)
+            ring = lax.rem(p, AHEAD)
+
+            @pl.when(p + AHEAD - 1 < pairs)
             def _():
-                phase_copy(p + 1, 1 - slot).start()
-
-            phase_copy(p, slot).wait()
+                phase_copy(p + AHEAD - 1, lax.rem(p + AHEAD - 1, AHEAD)).start()
+
+            phase_copy(p, ring).wait()
         else:
+            ring = slot
             spot = spot_ref[slot]
             if keep:
 
@@ -461,7 +468,7 @@
                 phase_ref[slot, first : first + value.shape[0], :] = value
 
             phase_rows(table_ref, spot[0:1], spot[1:2], spot[2:3], put)
-        factor_ref[...] += mm(phase_ref[slot], charge)
+        factor_ref[...] += mm(phase_ref[ring], charge)
         if keep and not reuse:
             phase_copy(p, slot).start()
         prepare(jnp.minimum(p + 1, pairs - 1))
@@ -514,13 +521,15 @@
     nx = lax.axis_size("gx")
     ny = lax.axis_size("gy")
     waves = wave_index.shape[1]
-    assert atoms == LANES and channels == LANES and waves % 64 == 0
+    assert atoms == channels == filter_weight.shape[1] == LANES and waves % 64 == 0
     state = features.reshape(atoms, channels)
+    weights = jnp.concatenate([input_weight, filter_weight, middle_weight, output_weight], axis=0)
     payload = pl.pallas_call(
         pack_kernel,
         out_shape=jax.ShapeDtypeStruct((atoms + GEO, channels), bf16),
         in_specs=[smem(), vmem(), vmem()],
         out_specs=vmem(),
+        compiler_params=pltpu.CompilerParams(vmem_limit_bytes=4 * 2**20),
         name="pack",
     )(counts, features, offsets.reshape(3, atoms))
 
@@ -535,7 +544,7 @@
     conv_call = lambda index: pl.pallas_call(
         functools.partial(conv_kernel, depth, slots, nx, ny, rows_of, index),
         out_shape=jax.ShapeDtypeStruct((atoms, channels), f32),
-        in_specs=[vmem() for _ in range(10)],
+        in_specs=[vmem() for _ in range(7)],
         out_specs=vmem(),
         scratch_shapes=[
             pltpu.VMEM((columns * atoms, 2 * channels), bf16),
@@ -548,6 +557,7 @@
             pltpu.VMEM((atoms, channels), f32),
             pltpu.VMEM((depth, CHUNK, channels), bf16),
         ],
+        compiler_params=pltpu.CompilerParams(vmem_limit_bytes=16 * 2**20),
         cost_estimate=pl.CostEstimate(flops=40_000_000_000, transcendentals=0, bytes_accessed=2_000_000),
         name="conv",
     )
@@ -555,6 +565,7 @@
     most_pairs = -(-everyone * atoms // CHUNK)
     keep = most_pairs * 2 * waves * CHUNK * 2 <= 16 * 2**20
     most_rows = most_pairs * CHUNK + slots
+    room = min((12 + everyone // 3) * 2**20, 60 * 2**20)
 
     def ewald_call(index, *operands):
         reuse = keep and index > 0
@@ -588,13 +599,14 @@
             scratch_shapes=geometry
             + [
                 pltpu.VMEM((3, waves, LANES), f32),
-                pltpu.VMEM((2, 2 * waves, CHUNK), bf16),
+                pltpu.VMEM((AHEAD if reuse else 2, 2 * waves, CHUNK), bf16),
                 pltpu.VMEM((2 * waves, channels), f32),
                 pltpu.VMEM((waves, channels), f32),
                 pltpu.VMEM((most_rows, channels), f32),
                 pltpu.VMEM((2, CHUNK, channels), bf16),
-                pltpu.SemaphoreType.DMA((2,)),
+                pltpu.SemaphoreType.DMA((AHEAD if reuse else 2,)),
             ],
+            compiler_params=pltpu.CompilerParams(vmem_limit_bytes=room),
             cost_estimate=pl.CostEstimate(flops=30_000_000_000, transcendentals=0, bytes_accessed=4_000_000),
             name="ewald",
         )(*operands)
@@ -613,10 +625,7 @@
             state_planes[0],
             state_planes[1],
             state_planes[nx - 1],
-            input_weight,
-            filter_weight,
-            middle_weight,
-            output_weight,
+            weights,
         )
         common = (state, conv, charge_weight, ewald_weight)
         if block == 0:

time: 87 us -> 74.7 us (0.86)
  Pallas kernels: 43.7 us -> 35.3 us
  other arithmetic: 3.12 us -> 0.07 us
  waiting for transfers between devices: 18.2 us -> 15.2 us
  local copies, waits for them, and re-layouts: 4.16 us -> 5.81 us
    pallas_call x2, Pallas kernels: 28.2 us -> 24 us  [shards(): conv_call(block)]
    pallas_call x2, Pallas kernels: 14.1 us -> 10.7 us  [ewald_call(): pl.pallas_call(functools.partial(ewald_kernel, depth, everyone * atoms, i...]
    ppermute x20, waiting for transfers between devices: 18.2 us -> 15.2 us  [gathered(): lax.ppermute(rows, axis, [(i, (i + shift) % size) for i in range(size)])]
    unnamed x2, other arithmetic: 1.55 us -> 0.03 us
    another operation x2, other arithmetic: 1.56 us -> 0.04 us  [spread_out(): return gathered(jnp.stack(gathered(rows, 'gy')), 'gx')]
    unnamed x31 -> x30, local copies, waits for them, and re-layouts: 4.12 us -> 4.92 us
  transfers between devices with their start and end apart: 20 -> 20, of which waited for: 11 -> 10; matrix products, arithmetic and copies ran while one was open for 3% -> 5% of each run, Pallas kernels for 16% -> 16%
where the time goes in v2:
time: 74.7 us; the launch traced here: 74.3 us
  Pallas kernels  35.3 us (47%)
  starting transfers between devices  17.7 us (24%)
  waiting for transfers between devices  15.2 us (20%)
  local copies, waits for them, and re-layouts  5.81 us (8%)
    pallas_call x2, Pallas kernels, shards(): conv_call(block)  24 us
    ppermute x20, starting transfers between devices, gathered(): lax.ppermute(rows, axis, [(i, (i + shift) % size) for i in range(size)])  17.7 us
    ppermute x20, waiting for transfers between devices, gathered(): lax.ppermute(rows, axis, [(i, (i + shift) % size) for i in range(size)])  15.2 us
    pallas_call x2, Pallas kernels, ewald_call(): pl.pallas_call(functools.partial(ewald_kernel, depth, everyone * atoms, i...  10.7 us
    unnamed x30, local copies, waits for them, and re-layouts  4.92 us
  transfers between devices with their start and end apart: 20, of which 10 were waited for; matrix products, arithmetic and copies ran while one was open for 5% of the time, Pallas kernels for 16%

profile of v2, /device:TPU:29, one launch (start us, length us, event | category | flops | bytes accessed | tf_op | source)
XLA Modules:
  0.0 74.3 jit_solution(4490387557786525306)
XLA Ops:
  0.0 0.7 copy.14
  0.7 0.8 %copy-done = bf16[1,1,128,128]{3,2,1,0:T(8,128)(2,1)S(1)} copy-done((bf16[1,1,128,128]{3,2,1,0:T(8,128)(2,1)S(1)}, bf16[1,1,128,128]{3,2,1,0:T(8,128)(2,1)}, u32[]{:S(2)}) %copy-start) | copy-done | bytes 32792
  1.4 0.7 copy-done.2
  2.1 0.6 pack.1
  2.7 0.1 collective-permute-start
  2.7 1.3 %collective-permute-start.1 = (bf16[144,128]{1,0:T(8,128)(2,1)S(1)}, bf16[144,128]{1,0:T(8,128)(2,1)S(1)}, u32[]{:S(2)}, u32[]{:S(2)}) collective-permute-start(bf16[144,128]{1,0:T(8,128)(2,1)S(1)} %pack.1), channel_id=1, source_target_pairs={{0,2},{1,3},{2,0},{3,1},{4,6},{5,7},{6,4},{7,5},{8,10},{9,11},{10,... | collective-permute-start | bytes 110600 | tf_op jit(solution)/shard_map/ppermute | solution.py:500
  4.1 0.2 collective-permute-start.2
  4.2 0.8 %constant_dynamic-update-slice_fusion.3 = bf16[8,128,128]{2,1,0:T(8,128)(2,1)S(1)} fusion(bf16[2,128,128]{2,1,0:T(8,128)(2,1)} %param.18), kind=kLoop, calls=%fused_computation.21 | loop fusion | bytes 131072
  5.1 0.9 %constant_dynamic-update-slice_fusion.2 = bf16[8,128,128]{2,1,0:T(8,128)(2,1)S(1)} fusion(bf16[8,128,128]{2,1,0:T(8,128)(2,1)S(1)} %constant_dynamic-update-slice_fusion.3, bf16[2,128,128]{2,1,0:T(8,128)(2,1)} %param.19), kind=kLoop, calls=%fused_computation.20 | loop fusion | bytes 131072
  5.9 0.9 %constant_dynamic-update-slice_fusion.1 = bf16[8,128,128]{2,1,0:T(8,128)(2,1)S(1)} fusion(bf16[8,128,128]{2,1,0:T(8,128)(2,1)S(1)} %constant_dynamic-update-slice_fusion.2, bf16[2,128,128]{2,1,0:T(8,128)(2,1)} %param.20), kind=kLoop, calls=%fused_computation.19 | loop fusion | bytes 131072
  6.8 0.0 collective-permute-done
  6.8 0.1 collective-permute-done.1
  6.9 1.9 %collective-permute-done.2 = bf16[144,128]{1,0:T(8,128)(2,1)S(1)} collective-permute-done((bf16[144,128]{1,0:T(8,128)(2,1)S(1)}, bf16[144,128]{1,0:T(8,128)(2,1)S(1)}, u32[]{:S(2)}, u32[]{:S(2)}) %collective-permute-start.2) | collective-permute-done | bytes 36896 | tf_op jit(solution)/shard_map/ppermute | solution.py:500
  8.7 3.5 %collective-permute-start.3 = (bf16[4,144,128]{2,1,0:T(8,128)(2,1)S(1)}, bf16[4,144,128]{2,1,0:T(8,128)(2,1)S(1)}, u32[]{:S(2)}, u32[]{:S(2)}) collective-permute-start(bf16[4,144,128]{2,1,0:T(8,128)(2,1)S(1)} %pad_maximum_fusion.geo_a.state_a), channel_id=1, source_target_pairs={{0,4},{4,8},{8,12},{12,16},{16,20},{20,24},{24,28},{28,0},{1,5},{5... | collective-permute-start | bytes 442376 | tf_op jit(solution)/shard_map/ppermute | solution.py:500
  12.2 0.9 %constant_dynamic-update-slice_fusion.weight_all_ref = bf16[8,128,128]{2,1,0:T(8,128)(2,1)S(1)} fusion(bf16[8,128,128]{2,1,0:T(8,128)(2,1)S(1)} %constant_dynamic-update-slice_fusion.1, bf16[2,128,128]{2,1,0:T(8,128)(2,1)} %param.21), kind=kLoop, calls=%fused_computation.18 | loop fusion | bytes 131072 | tf_op jit(solution)/shard_map/concatenate | solution.py:526
  13.1 0.2 collective-permute-start.4
  13.3 0.3 collective-permute-start.5
  13.7 1.2 %collective-permute-start.6 = (bf16[4,144,128]{2,1,0:T(8,128)(2,1)S(1)}, bf16[4,144,128]{2,1,0:T(8,128)(2,1)S(1)}, u32[]{:S(2)}, u32[]{:S(2)}) collective-permute-start(bf16[4,144,128]{2,1,0:T(8,128)(2,1)S(1)} %pad_maximum_fusion.geo_a.state_a), channel_id=1, source_target_pairs={{0,16},{4,20},{8,24},{12,28},{16,0},{20,4},{24,8},{28,12},{1,17},{... | collective-permute-start | bytes 442376 | tf_op jit(solution)/shard_map/ppermute | solution.py:500
  14.9 2.6 %collective-permute-start.7 = (bf16[4,144,128]{2,1,0:T(8,128)(2,1)S(1)}, bf16[4,144,128]{2,1,0:T(8,128)(2,1)S(1)}, u32[]{:S(2)}, u32[]{:S(2)}) collective-permute-start(bf16[4,144,128]{2,1,0:T(8,128)(2,1)S(1)} %pad_maximum_fusion.geo_a.state_a), channel_id=1, source_target_pairs={{0,20},{4,24},{8,28},{12,0},{16,4},{20,8},{24,12},{28,16},{1,21},{... | collective-permute-start | bytes 442376 | tf_op jit(solution)/shard_map/ppermute | solution.py:500
  17.5 0.0 collective-permute-done.3.geo_b.state_b
  17.5 0.3 collective-permute-start.8
  17.9 1.8 %collective-permute-done.4 = bf16[4,144,128]{2,1,0:T(8,128)(2,1)S(1)} collective-permute-done((bf16[4,144,128]{2,1,0:T(8,128)(2,1)S(1)}, bf16[4,144,128]{2,1,0:T(8,128)(2,1)S(1)}, u32[]{:S(2)}, u32[]{:S(2)}) %collective-permute-start.4) | collective-permute-done | bytes 147488 | tf_op jit(solution)/shard_map/ppermute | solution.py:500
  19.7 2.3 %collective-permute-done.5 = bf16[4,144,128]{2,1,0:T(8,128)(2,1)S(1)} collective-permute-done((bf16[4,144,128]{2,1,0:T(8,128)(2,1)S(1)}, bf16[4,144,128]{2,1,0:T(8,128)(2,1)S(1)}, u32[]{:S(2)}, u32[]{:S(2)}) %collective-permute-start.5) | collective-permute-done | bytes 147488 | tf_op jit(solution)/shard_map/ppermute | solution.py:500
  22.1 4.8 %collective-permute-done.6 = bf16[4,144,128]{2,1,0:T(8,128)(2,1)S(1)} collective-permute-done((bf16[4,144,128]{2,1,0:T(8,128)(2,1)S(1)}, bf16[4,144,128]{2,1,0:T(8,128)(2,1)S(1)}, u32[]{:S(2)}, u32[]{:S(2)}) %collective-permute-start.6) | collective-permute-done | bytes 147488 | tf_op jit(solution)/shard_map/ppermute | solution.py:500
  26.9 0.1 collective-permute-done.7
  27.1 0.0 copy-start.1
  27.1 0.0 copy-start.3
  27.1 0.0 copy-start.4
  27.1 0.0 copy-start.5
  27.1 0.0 copy-start.6
  27.1 12.0 %conv.2.refs_4_ = f32[128,128]{1,0:T(8,128)S(1)} custom-call(bf16[4,144,128]{2,1,0:T(8,128)(2,1)S(1)} %pad_maximum_fusion.geo_a.state_a, bf16[4,144,128]{2,1,0:T(8,128)(2,1)S(1)} %collective-permute-done.3.geo_b.state_b, bf16[4,144,128]{2,1,0:T(8,128)(2,1)S(1)} %collective-permute-done.9.geo_c.state_c, ...), custom_call_target="tpu_custom_call" | custom-call | flops 40000000000 | bytes 2000000 | tf_op jit(solution)/shard_map/conv/pallas_call | solution.py:621
  39.2 6.5 %ewald.2 = (bf16[128,128]{1,0:T(8,128)(2,1)S(1)}, s32[40,128]{1,0:T(8,128)S(1)}, bf16[1024,128]{1,0:T(8,128)(2,1)S(1)}, bf16[16,1024,256]{2,1,0:T(8,128)(2,1)S(1)}) custom-call(s32[3,512]{1,0:T(4,128)S(1)} %copy-done.5, f32[2,128]{1,0:T(2,128)S(1)} %copy-done.6, bf16[8,4,144,128]{3,2,1,0:T(8,128)(2,1)S(1)} %bitcast_dynamic-update-slice_fusion.refs_2_, ...), custom_call_target="tpu_custom_call" | custom-call | flops 30000001024 | bytes 4000000 | tf_op jit(solution)/shard_map/ewald/pallas_call | solution.py:594
  45.7 0.1 collective-permute-start.10
  45.8 0.1 collective-permute-start.11
  45.9 1.4 %collective-permute-start.12 = (bf16[128,128]{1,0:T(8,128)(2,1)S(1)}, bf16[128,128]{1,0:T(8,128)(2,1)S(1)}, u32[]{:S(2)}, u32[]{:S(2)}) collective-permute-start(bf16[128,128]{1,0:T(8,128)(2,1)S(1)} %get-tuple-element.12.refs_6_), channel_id=1, source_target_pairs={{0,3},{1,0},{2,1},{3,2},{4,7},{5,4},{6,5},{7,6},{8,11},{9,8},{10,9... | collective-permute-start | bytes 98312 | tf_op jit(solution)/shard_map/ppermute | solution.py:500
  47.3 1.3 %collective-permute-done.10 = bf16[128,128]{1,0:T(8,128)(2,1)S(1)} collective-permute-done((bf16[128,128]{1,0:T(8,128)(2,1)S(1)}, bf16[128,128]{1,0:T(8,128)(2,1)S(1)}, u32[]{:S(2)}, u32[]{:S(2)}) %collective-permute-start.10) | collective-permute-done | bytes 32800 | tf_op jit(solution)/shard_map/ppermute | solution.py:500
  48.5 1.0 %collective-permute-done.11 = bf16[128,128]{1,0:T(8,128)(2,1)S(1)} collective-permute-done((bf16[128,128]{1,0:T(8,128)(2,1)S(1)}, bf16[128,128]{1,0:T(8,128)(2,1)S(1)}, u32[]{:S(2)}, u32[]{:S(2)}) %collective-permute-start.11) | collective-permute-done | bytes 32800 | tf_op jit(solution)/shard_map/ppermute | solution.py:500
  49.5 1.5 %collective-permute-done.12 = bf16[128,128]{1,0:T(8,128)(2,1)S(1)} collective-permute-done((bf16[128,128]{1,0:T(8,128)(2,1)S(1)}, bf16[128,128]{1,0:T(8,128)(2,1)S(1)}, u32[]{:S(2)}, u32[]{:S(2)}) %collective-permute-start.12) | collective-permute-done | bytes 32800 | tf_op jit(solution)/shard_map/ppermute | solution.py:500
  51.0 0.1 collective-permute-start.13
  51.1 0.5 collective-permute-start.19
  51.6 1.1 %collective-permute-start.15 = (bf16[4,128,128]{2,1,0:T(8,128)(2,1)S(1)}, bf16[4,128,128]{2,1,0:T(8,128)(2,1)S(1)}, u32[]{:S(2)}, u32[]{:S(2)}) collective-permute-start(bf16[4,128,128]{2,1,0:T(8,128)(2,1)S(1)} %pad_maximum_fusion.1.state_a), channel_id=1, source_target_pairs={{0,12},{4,16},{8,20},{12,24},{16,28},{20,0},{24,4},{28,8},{1,13},{... | collective-permute-start | bytes 393224 | tf_op jit(solution)/shard_map/ppermute | solution.py:500
  52.6 2.0 %collective-permute-start.16 = (bf16[4,128,128]{2,1,0:T(8,128)(2,1)S(1)}, bf16[4,128,128]{2,1,0:T(8,128)(2,1)S(1)}, u32[]{:S(2)}, u32[]{:S(2)}) collective-permute-start(bf16[4,128,128]{2,1,0:T(8,128)(2,1)S(1)} %pad_maximum_fusion.1.state_a), channel_id=1, source_target_pairs={{0,16},{4,20},{8,24},{12,28},{16,0},{20,4},{24,8},{28,12},{1,17},{... | collective-permute-start | bytes 393224 | tf_op jit(solution)/shard_map/ppermute | solution.py:500
  54.6 0.0 collective-permute-done.13.state_b
  54.6 0.7 collective-permute-start.17
  55.4 0.5 collective-permute-done.19.state_c
  55.8 2.0 %collective-permute-start.18 = (bf16[4,128,128]{2,1,0:T(8,128)(2,1)S(1)}, bf16[4,128,128]{2,1,0:T(8,128)(2,1)S(1)}, u32[]{:S(2)}, u32[]{:S(2)}) collective-permute-start(bf16[4,128,128]{2,1,0:T(8,128)(2,1)S(1)} %pad_maximum_fusion.1.state_a), channel_id=1, source_target_pairs={{0,24},{4,28},{8,0},{12,4},{16,8},{20,12},{24,16},{28,20},{1,25},{... | collective-permute-start | bytes 393224 | tf_op jit(solution)/shard_map/ppermute | solution.py:500
  57.9 12.0 %conv.3.refs_7_ = f32[128,128]{1,0:T(8,128)S(1)} custom-call(bf16[4,144,128]{2,1,0:T(8,128)(2,1)S(1)} %pad_maximum_fusion.geo_a.state_a, bf16[4,144,128]{2,1,0:T(8,128)(2,1)S(1)} %collective-permute-done.3.geo_b.state_b, bf16[4,144,128]{2,1,0:T(8,128)(2,1)S(1)} %collective-permute-done.9.geo_c.state_c, bf16[4,128,128]{2,1,0:T(8,128)(2,1)S(1)} %pad_maximum_fusion.1.state_a, ...), custom_call_target="tpu_custom_call" | custom-call | flops 40000000000 | bytes 2000000 | tf_op jit(solution)/shard_map/conv/pallas_call | solution.py:621
  70.1 4.2 %ewald.3 = bf16[128,128]{1,0:T(8,128)(2,1)} custom-call(s32[40,128]{1,0:T(8,128)S(1)} %get-tuple-element.9.refs_0_, bf16[1024,128]{1,0:T(8,128)(2,1)S(1)} %get-tuple-element.10.refs_1_, bf16[16,1024,256]{2,1,0:T(8,128)(2,1)S(1)} %get-tuple-element.11.refs_2_, s32[3,512]{1,0:T(4,128)S(1)} %copy-done.5, f32[2,128]{1,0:T(2,128)S(1)} %copy-done.6, ...), custom_call_target="tpu_custom_call" | custom-call | flops 30000001024 | bytes 4000000 | tf_op jit(solution)/shard_map/ewald/pallas_call | solution.py:594
  (34 shorter events, 0.4 us)
Async XLA Ops:
  0.7 0.8 %copy-start = (bf16[1,1,128,128]{3,2,1,0:T(8,128)(2,1)S(1)}, bf16[1,1,128,128]{3,2,1,0:T(8,128)(2,1)}, u32[]{:S(2)}) copy-start(bf16[1,1,128,128]{3,2,1,0:T(8,128)(2,1)} %features_ref.1) | copy-start | bytes 98308
  1.4 0.7 copy-start.2
  2.7 4.1 %collective-permute-start = (bf16[144,128]{1,0:T(8,128)(2,1)S(1)}, bf16[144,128]{1,0:T(8,128)(2,1)S(1)}, u32[]{:S(2)}, u32[]{:S(2)}) collective-permute-start(bf16[144,128]{1,0:T(8,128)(2,1)S(1)} %pack.1), channel_id=1, source_target_pairs={{0,1},{1,2},{2,3},{3,0},{4,5},{5,6},{6,7},{7,4},{8,9},{9,10},{10,1... | collective-permute-start | bytes 110600 | tf_op jit(solution)/shard_map/ppermute | solution.py:500
  2.7 4.1 %collective-permute-start.1 = (bf16[144,128]{1,0:T(8,128)(2,1)S(1)}, bf16[144,128]{1,0:T(8,128)(2,1)S(1)}, u32[]{:S(2)}, u32[]{:S(2)}) collective-permute-start(bf16[144,128]{1,0:T(8,128)(2,1)S(1)} %pack.1), channel_id=1, source_target_pairs={{0,2},{1,3},{2,0},{3,1},{4,6},{5,7},{6,4},{7,5},{8,10},{9,11},{10,... | collective-permute-start | bytes 110600 | tf_op jit(solution)/shard_map/ppermute | solution.py:500
  4.1 4.7 %collective-permute-start.2 = (bf16[144,128]{1,0:T(8,128)(2,1)S(1)}, bf16[144,128]{1,0:T(8,128)(2,1)S(1)}, u32[]{:S(2)}, u32[]{:S(2)}) collective-permute-start(bf16[144,128]{1,0:T(8,128)(2,1)S(1)} %pack.1), channel_id=1, source_target_pairs={{0,3},{1,0},{2,1},{3,2},{4,7},{5,4},{6,5},{7,6},{8,11},{9,8},{10,9... | collective-permute-start | bytes 110600 | tf_op jit(solution)/shard_map/ppermute | solution.py:500
  8.7 8.8 %collective-permute-start.3 = (bf16[4,144,128]{2,1,0:T(8,128)(2,1)S(1)}, bf16[4,144,128]{2,1,0:T(8,128)(2,1)S(1)}, u32[]{:S(2)}, u32[]{:S(2)}) collective-permute-start(bf16[4,144,128]{2,1,0:T(8,128)(2,1)S(1)} %pad_maximum_fusion.geo_a.state_a), channel_id=1, source_target_pairs={{0,4},{4,8},{8,12},{12,16},{16,20},{20,24},{24,28},{28,0},{1,5},{5... | collective-permute-start | bytes 442376 | tf_op jit(solution)/shard_map/ppermute | solution.py:500
  13.1 6.6 %collective-permute-start.4 = (bf16[4,144,128]{2,1,0:T(8,128)(2,1)S(1)}, bf16[4,144,128]{2,1,0:T(8,128)(2,1)S(1)}, u32[]{:S(2)}, u32[]{:S(2)}) collective-permute-start(bf16[4,144,128]{2,1,0:T(8,128)(2,1)S(1)} %pad_maximum_fusion.geo_a.state_a), channel_id=1, source_target_pairs={{0,8},{4,12},{8,16},{12,20},{16,24},{20,28},{24,0},{28,4},{1,9},{5... | collective-permute-start | bytes 442376 | tf_op jit(solution)/shard_map/ppermute | solution.py:500
  13.3 8.7 %collective-permute-start.5 = (bf16[4,144,128]{2,1,0:T(8,128)(2,1)S(1)}, bf16[4,144,128]{2,1,0:T(8,128)(2,1)S(1)}, u32[]{:S(2)}, u32[]{:S(2)}) collective-permute-start(bf16[4,144,128]{2,1,0:T(8,128)(2,1)S(1)} %pad_maximum_fusion.geo_a.state_a), channel_id=1, source_target_pairs={{0,12},{4,16},{8,20},{12,24},{16,28},{20,0},{24,4},{28,8},{1,13},{... | collective-permute-start | bytes 442376 | tf_op jit(solution)/shard_map/ppermute | solution.py:500
  13.7 13.2 %collective-permute-start.6 = (bf16[4,144,128]{2,1,0:T(8,128)(2,1)S(1)}, bf16[4,144,128]{2,1,0:T(8,128)(2,1)S(1)}, u32[]{:S(2)}, u32[]{:S(2)}) collective-permute-start(bf16[4,144,128]{2,1,0:T(8,128)(2,1)S(1)} %pad_maximum_fusion.geo_a.state_a), channel_id=1, source_target_pairs={{0,16},{4,20},{8,24},{12,28},{16,0},{20,4},{24,8},{28,12},{1,17},{... | collective-permute-start | bytes 442376 | tf_op jit(solution)/shard_map/ppermute | solution.py:500
  14.9 12.1 %collective-permute-start.7 = (bf16[4,144,128]{2,1,0:T(8,128)(2,1)S(1)}, bf16[4,144,128]{2,1,0:T(8,128)(2,1)S(1)}, u32[]{:S(2)}, u32[]{:S(2)}) collective-permute-start(bf16[4,144,128]{2,1,0:T(8,128)(2,1)S(1)} %pad_maximum_fusion.geo_a.state_a), channel_id=1, source_target_pairs={{0,20},{4,24},{8,28},{12,0},{16,4},{20,8},{24,12},{28,16},{1,21},{... | collective-permute-start | bytes 442376 | tf_op jit(solution)/shard_map/ppermute | solution.py:500
  17.5 9.5 %collective-permute-start.8 = (bf16[4,144,128]{2,1,0:T(8,128)(2,1)S(1)}, bf16[4,144,128]{2,1,0:T(8,128)(2,1)S(1)}, u32[]{:S(2)}, u32[]{:S(2)}) collective-permute-start(bf16[4,144,128]{2,1,0:T(8,128)(2,1)S(1)} %pad_maximum_fusion.geo_a.state_a), channel_id=1, source_target_pairs={{0,24},{4,28},{8,0},{12,4},{16,8},{20,12},{24,16},{28,20},{1,25},{... | collective-permute-start | bytes 442376 | tf_op jit(solution)/shard_map/ppermute | solution.py:500
  19.7 7.3 %collective-permute-start.9 = (bf16[4,144,128]{2,1,0:T(8,128)(2,1)S(1)}, bf16[4,144,128]{2,1,0:T(8,128)(2,1)S(1)}, u32[]{:S(2)}, u32[]{:S(2)}) collective-permute-start(bf16[4,144,128]{2,1,0:T(8,128)(2,1)S(1)} %pad_maximum_fusion.geo_a.state_a), channel_id=1, source_target_pairs={{0,28},{4,0},{8,4},{12,8},{16,12},{20,16},{24,20},{28,24},{1,29},{... | collective-permute-start | bytes 442376 | tf_op jit(solution)/shard_map/ppermute | solution.py:500
  27.1 12.1 %copy-start.1 = (bf16[1,1,128,128]{3,2,1,0:T(8,128)(2,1)S(1)}, bf16[1,1,128,128]{3,2,1,0:T(8,128)(2,1)}, u32[]{:S(2)}) copy-start(bf16[1,1,128,128]{3,2,1,0:T(8,128)(2,1)} %features_ref.1) | copy-start | bytes 98308
  27.1 12.1 %copy-start.3 = (bf16[2,128,128]{2,1,0:T(8,128)(2,1)S(1)}, bf16[2,128,128]{2,1,0:T(8,128)(2,1)}, u32[]{:S(2)}) copy-start(bf16[2,128,128]{2,1,0:T(8,128)(2,1)} %refs_8_.1) | copy-start | bytes 196612
  27.1 12.1 %copy-start.4 = (bf16[2,128,128]{2,1,0:T(8,128)(2,1)S(1)}, bf16[2,128,128]{2,1,0:T(8,128)(2,1)}, u32[]{:S(2)}) copy-start(bf16[2,128,128]{2,1,0:T(8,128)(2,1)} %refs_9_.1) | copy-start | bytes 196612
  27.1 12.1 %copy-start.5 = (s32[3,512]{1,0:T(4,128)S(1)}, s32[3,512]{1,0:T(4,128)}, u32[]{:S(2)}) copy-start(s32[3,512]{1,0:T(4,128)} %refs_3_.1) | copy-start | bytes 18436
  27.1 12.1 %copy-start.6 = (f32[2,128]{1,0:T(2,128)S(1)}, f32[2,128]{1,0:T(2,128)}, u32[]{:S(2)}) copy-start(f32[2,128]{1,0:T(2,128)} %refs_4_.1) | copy-start | bytes 3076
  45.7 2.8 %collective-permute-start.10 = (bf16[128,128]{1,0:T(8,128)(2,1)S(1)}, bf16[128,128]{1,0:T(8,128)(2,1)S(1)}, u32[]{:S(2)}, u32[]{:S(2)}) collective-permute-start(bf16[128,128]{1,0:T(8,128)(2,1)S(1)} %get-tuple-element.12.refs_6_), channel_id=1, source_target_pairs={{0,1},{1,2},{2,3},{3,0},{4,5},{5,6},{6,7},{7,4},{8,9},{9,10},{10,1... | collective-permute-start | bytes 98312 | tf_op jit(solution)/shard_map/ppermute | solution.py:500
  45.8 3.7 %collective-permute-start.11 = (bf16[128,128]{1,0:T(8,128)(2,1)S(1)}, bf16[128,128]{1,0:T(8,128)(2,1)S(1)}, u32[]{:S(2)}, u32[]{:S(2)}) collective-permute-start(bf16[128,128]{1,0:T(8,128)(2,1)S(1)} %get-tuple-element.12.refs_6_), channel_id=1, source_target_pairs={{0,2},{1,3},{2,0},{3,1},{4,6},{5,7},{6,4},{7,5},{8,10},{9,11},{10,... | collective-permute-start | bytes 98312 | tf_op jit(solution)/shard_map/ppermute | solution.py:500
  45.9 5.1 %collective-permute-start.12 = (bf16[128,128]{1,0:T(8,128)(2,1)S(1)}, bf16[128,128]{1,0:T(8,128)(2,1)S(1)}, u32[]{:S(2)}, u32[]{:S(2)}) collective-permute-start(bf16[128,128]{1,0:T(8,128)(2,1)S(1)} %get-tuple-element.12.refs_6_), channel_id=1, source_target_pairs={{0,3},{1,0},{2,1},{3,2},{4,7},{5,4},{6,5},{7,6},{8,11},{9,8},{10,9... | collective-permute-start | bytes 98312 | tf_op jit(solution)/shard_map/ppermute | solution.py:500
  51.0 3.6 %collective-permute-start.13 = (bf16[4,128,128]{2,1,0:T(8,128)(2,1)S(1)}, bf16[4,128,128]{2,1,0:T(8,128)(2,1)S(1)}, u32[]{:S(2)}, u32[]{:S(2)}) collective-permute-start(bf16[4,128,128]{2,1,0:T(8,128)(2,1)S(1)} %pad_maximum_fusion.1.state_a), channel_id=1, source_target_pairs={{0,4},{4,8},{8,12},{12,16},{16,20},{20,24},{24,28},{28,0},{1,5},{5... | collective-permute-start | bytes 393224 | tf_op jit(solution)/shard_map/ppermute | solution.py:500
  51.1 4.8 %collective-permute-start.19 = (bf16[4,128,128]{2,1,0:T(8,128)(2,1)S(1)}, bf16[4,128,128]{2,1,0:T(8,128)(2,1)S(1)}, u32[]{:S(2)}, u32[]{:S(2)}) collective-permute-start(bf16[4,128,128]{2,1,0:T(8,128)(2,1)S(1)} %pad_maximum_fusion.1.state_a), channel_id=1, source_target_pairs={{0,28},{4,0},{8,4},{12,8},{16,12},{20,16},{24,20},{28,24},{1,29},{... | collective-permute-start | bytes 393224 | tf_op jit(solution)/shard_map/ppermute | solution.py:500
  51.6 18.4 %collective-permute-start.14 = (bf16[4,128,128]{2,1,0:T(8,128)(2,1)S(1)}, bf16[4,128,128]{2,1,0:T(8,128)(2,1)S(1)}, u32[]{:S(2)}, u32[]{:S(2)}) collective-permute-start(bf16[4,128,128]{2,1,0:T(8,128)(2,1)S(1)} %pad_maximum_fusion.1.state_a), channel_id=1, source_target_pairs={{0,8},{4,12},{8,16},{12,20},{16,24},{20,28},{24,0},{28,4},{1,9},{5... | collective-permute-start | bytes 393224 | tf_op jit(solution)/shard_map/ppermute | solution.py:500
  51.6 18.4 %collective-permute-start.15 = (bf16[4,128,128]{2,1,0:T(8,128)(2,1)S(1)}, bf16[4,128,128]{2,1,0:T(8,128)(2,1)S(1)}, u32[]{:S(2)}, u32[]{:S(2)}) collective-permute-start(bf16[4,128,128]{2,1,0:T(8,128)(2,1)S(1)} %pad_maximum_fusion.1.state_a), channel_id=1, source_target_pairs={{0,12},{4,16},{8,20},{12,24},{16,28},{20,0},{24,4},{28,8},{1,13},{... | collective-permute-start | bytes 393224 | tf_op jit(solution)/shard_map/ppermute | solution.py:500
  52.6 17.4 %collective-permute-start.16 = (bf16[4,128,128]{2,1,0:T(8,128)(2,1)S(1)}, bf16[4,128,128]{2,1,0:T(8,128)(2,1)S(1)}, u32[]{:S(2)}, u32[]{:S(2)}) collective-permute-start(bf16[4,128,128]{2,1,0:T(8,128)(2,1)S(1)} %pad_maximum_fusion.1.state_a), channel_id=1, source_target_pairs={{0,16},{4,20},{8,24},{12,28},{16,0},{20,4},{24,8},{28,12},{1,17},{... | collective-permute-start | bytes 393224 | tf_op jit(solution)/shard_map/ppermute | solution.py:500
  54.6 15.4 %collective-permute-start.17 = (bf16[4,128,128]{2,1,0:T(8,128)(2,1)S(1)}, bf16[4,128,128]{2,1,0:T(8,128)(2,1)S(1)}, u32[]{:S(2)}, u32[]{:S(2)}) collective-permute-start(bf16[4,128,128]{2,1,0:T(8,128)(2,1)S(1)} %pad_maximum_fusion.1.state_a), channel_id=1, source_target_pairs={{0,20},{4,24},{8,28},{12,0},{16,4},{20,8},{24,12},{28,16},{1,21},{... | collective-permute-start | bytes 393224 | tf_op jit(solution)/shard_map/ppermute | solution.py:500
  55.8 14.2 %collective-permute-start.18 = (bf16[4,128,128]{2,1,0:T(8,128)(2,1)S(1)}, bf16[4,128,128]{2,1,0:T(8,128)(2,1)S(1)}, u32[]{:S(2)}, u32[]{:S(2)}) collective-permute-start(bf16[4,128,128]{2,1,0:T(8,128)(2,1)S(1)} %pad_maximum_fusion.1.state_a), channel_id=1, source_target_pairs={{0,24},{4,28},{8,0},{12,4},{16,8},{20,12},{24,16},{28,20},{1,25},{... | collective-permute-start | bytes 393224 | tf_op jit(solution)/shard_map/ppermute | solution.py:500

commit v3 on v2

--- a/solution.py
+++ b/solution.py
@@ -16,6 +16,7 @@
 GEO = 16
 LIVE, LOW, SLOT, MID, SPOT = 3, 4, 7, 8, 11
 CHUNK = 256
+WIDE = 384
 GROUP = 16
 NONE = -1.0e30
 INPUT, FILTER, MIDDLE, OUTPUT = range(4)
@@ -173,6 +174,8 @@
     center_ref,
     message_ref,
     mapped_ref,
+    target_ref,
+    total_ref,
 ):
     atoms, channels = message_ref.shape
     count = weight_all_ref.shape[1]
@@ -194,10 +197,10 @@
         if plane == 0:
             here_x = wide[SPOT : SPOT + 1, 0:1]
             here_y = wide[SPOT + 1 : SPOT + 2, 0:1]
-            target = [
-                (turned[:, a : a + 1] + turned[:, MID + a : MID + a + 1]) + turned[:, LOW + a : LOW + a + 1]
-                for a in range(3)
-            ]
+            for a in range(3):
+                target_ref[:, a : a + 1] = (
+                    turned[:, a : a + 1] + turned[:, MID + a : MID + a + 1]
+                ) + turned[:, LOW + a : LOW + a + 1]
         for i, row in enumerate(rows_of):
             part = slice((plane * near + i) * atoms, (plane * near + i + 1) * atoms)
             source_ref[part, 0:channels] = mm(state[plane][row, 0:atoms, :], weight_all_ref[input_at]).astype(bf16)
@@ -215,42 +218,47 @@
     layers = (iota((block, atoms), 1) // slots).astype(f32)
     lives = []
     longest = jnp.int32(0)
-    totals = []
     for cell in range(depth):
         out_z = outside(wrapped(layers - float(cell), depth) + z)
         close = jnp.where(flat + out_z * out_z < 1.001, live, 0.0)
         lives.append(close)
-        totals.append(jnp.sum(close).astype(jnp.int32))
-        longest = jnp.maximum(longest, totals[-1])
+        total = jnp.sum(close).astype(jnp.int32)
+        total_ref[cell] = total
+        longest = jnp.maximum(longest, total)
     place_ref[...] = places(jnp.concatenate(lives, axis=0), block)
-    center_ref[...] = iota((count, CHUNK), 0).astype(f32) * spread
+    center_ref[...] = iota((count, WIDE), 0).astype(f32) * spread
     wide_ref[...] = weight_all_ref[filter_at].astype(f32)
     message_ref[...] = jnp.zeros_like(message_ref)
     pick_rows = identity(near * GEO, atoms)
 
     def piece(first, width):
-        for cell in range(depth):
-            want = chosen(place_ref[cell * block : cell * block + columns, :], first, width)
+        def cell_step(cell, carry):
+            rows = pl.ds(pl.multiple_of(cell * block, block), block)
+            want = chosen(place_ref[rows, :][0:columns], first, width)
             found = mm(want, source_ref[...])
             mapped_ref[cell, 0:width, :] = found[:, 0:channels].astype(bf16)
             known = grouped(mm_nt(pick_rows, found[:, channels : 2 * channels].astype(bf16)), near)
-            part = slice(cell * slots, (cell + 1) * slots)
+            part = pl.ds(pl.multiple_of(cell * slots, slots), slots)
             along_x = wrapped(known[SPOT : SPOT + 1] - here_x, size_x)
             along_y = wrapped(known[SPOT + 1 : SPOT + 2] - here_y, size_y)
-            along_z = wrapped(known[SPOT + 2 : SPOT + 3] - float(cell), depth)
+            along_z = wrapped(known[SPOT + 2 : SPOT + 3] - cell.astype(f32), depth)
             home = jnp.abs(along_x) + jnp.abs(along_y)
             who = jnp.where(home == 0.0, known[SLOT : SLOT + 1], 0.0)
-            diff_x = (along_x + joined(known, 0)) - target[0][part, :]
-            diff_y = (along_y + joined(known, 1)) - target[1][part, :]
-            diff_z = (along_z + joined(known, 2)) - target[2][part, :]
+            target = target_ref[part, :]
+            diff_x = (along_x + joined(known, 0)) - target[:, 0:1]
+            diff_y = (along_y + joined(known, 1)) - target[:, 1:2]
+            diff_z = (along_z + joined(known, 2)) - target[:, 2:3]
             square = diff_x * diff_x + diff_y * diff_y + diff_z * diff_z
             dist = jnp.sqrt(square)
             mine = (iota((slots, width), 0) + (cell * slots + 1)).astype(f32)
             kept = jnp.logical_and(dist < 1.0, who != mine)
-            kept = jnp.logical_and(kept, iota((slots, width), 1) + first < totals[cell])
+            kept = jnp.logical_and(kept, iota((slots, width), 1) + first < total_ref[cell])
             half = jnp.maximum(power_sum(COS_HALF, jnp.minimum(square, 1.0)), 1.0e-18)
             weight_ref[part, 0:width] = jnp.where(kept, 2.0 * jnp.log2(half), NONE)
             scale_ref[part, 0:width] = dist * ((count - 1) * spread)
+            return carry
+
+        lax.fori_loop(0, depth, cell_step, 0)
 
         def group_step(g, carry):
             start = pl.multiple_of(g * GROUP, GROUP)
@@ -271,7 +279,9 @@
 
         lax.fori_loop(0, atoms // GROUP, group_step, 0)
 
-    full = (longest + (LANES - 1)) // CHUNK
+    tiles = (longest + (LANES - 1)) // LANES
+    odd = jnp.logical_and(lax.rem(tiles, 2) == 1, tiles >= 3)
+    full = (tiles + 1) // 2 - jnp.where(odd, 2, 0)
 
     def chunk_step(chunk, carry):
         piece(chunk * CHUNK, CHUNK)
@@ -279,9 +289,9 @@
 
     lax.fori_loop(0, full, chunk_step, 0)
 
-    @pl.when(full * CHUNK < longest)
+    @pl.when(odd)
     def _():
-        piece(full * CHUNK, LANES)
+        piece(full * CHUNK, WIDE)
 
     middle = silu(mm(message_ref[...].astype(bf16), weight_all_ref[middle_at])).astype(bf16)
     out_ref[...] = mm(middle, weight_all_ref[output_at])
@@ -549,13 +559,15 @@
         scratch_shapes=[
             pltpu.VMEM((columns * atoms, 2 * channels), bf16),
             pltpu.VMEM((depth * tall, atoms), f32),
-            pltpu.VMEM((atoms, CHUNK), f32),
-            pltpu.VMEM((atoms, CHUNK), f32),
-            pltpu.VMEM((GROUP * count, CHUNK), bf16),
+            pltpu.VMEM((atoms, WIDE), f32),
+            pltpu.VMEM((atoms, WIDE), f32),
+            pltpu.VMEM((GROUP * count, WIDE), bf16),
             pltpu.VMEM((count, channels), f32),
-            pltpu.VMEM((count, CHUNK), f32),
+            pltpu.VMEM((count, WIDE), f32),
             pltpu.VMEM((atoms, channels), f32),
-            pltpu.VMEM((depth, CHUNK, channels), bf16),
+            pltpu.VMEM((depth, WIDE, channels), bf16),
+            pltpu.VMEM((atoms, LANES), f32),
+            pltpu.SMEM((depth,), jnp.int32),
         ],
         compiler_params=pltpu.CompilerParams(vmem_limit_bytes=16 * 2**20),
         cost_estimate=pl.CostEstimate(flops=40_000_000_000, transcendentals=0, bytes_accessed=2_000_000),

time: 74.7 us -> 71.5 us (0.957)
  the two profiles are of different devices: /device:TPU:29 before, /device:TPU:0 now
where the time goes in v3:
time: 71.5 us; the launch traced here: 70.4 us
  starting transfers between devices  27.8 us (39%)
  Pallas kernels  25.7 us (36%)
  waiting for transfers between devices  10.6 us (15%)
  local copies, waits for them, and re-layouts  5.81 us (8%)
    ppermute x20, starting transfers between devices, gathered(): lax.ppermute(rows, axis, [(i, (i + shift) % size) for i in range(size)])  27.8 us
    pallas_call x2, Pallas kernels, shards(): conv_call(block)  14.5 us
    pallas_call x2, Pallas kernels, ewald_call(): pl.pallas_call(functools.partial(ewald_kernel, depth, everyone * atoms, i...  10.7 us
    ppermute x20, waiting for transfers between devices, gathered(): lax.ppermute(rows, axis, [(i, (i + shift) % size) for i in range(size)])  10.6 us
    unnamed x30, local copies, waits for them, and re-layouts  4.92 us
  transfers between devices with their start and end apart: 20, of which 8 were waited for; matrix products, arithmetic and copies ran while one was open for 5% of the time, Pallas kernels for 10%

profile of v3, /device:TPU:0, one launch (start us, length us, event | category | flops | bytes accessed | tf_op | source)
XLA Modules:
  0.0 70.4 jit_solution(12181582937857437343)
XLA Ops:
  0.0 0.7 copy.14
  0.7 0.8 %copy-done = bf16[1,1,128,128]{3,2,1,0:T(8,128)(2,1)S(1)} copy-done((bf16[1,1,128,128]{3,2,1,0:T(8,128)(2,1)S(1)}, bf16[1,1,128,128]{3,2,1,0:T(8,128)(2,1)}, u32[]{:S(2)}) %copy-start) | copy-done | bytes 32792
  1.4 0.7 copy-done.2
  2.1 0.6 pack.1
  2.7 3.1 %collective-permute-start = (bf16[144,128]{1,0:T(8,128)(2,1)S(1)}, bf16[144,128]{1,0:T(8,128)(2,1)S(1)}, u32[]{:S(2)}, u32[]{:S(2)}) collective-permute-start(bf16[144,128]{1,0:T(8,128)(2,1)S(1)} %pack.1), channel_id=1, source_target_pairs={{0,1},{1,2},{2,3},{3,0},{4,5},{5,6},{6,7},{7,4},{8,9},{9,10},{10,1... | collective-permute-start | bytes 110600 | tf_op jit(solution)/shard_map/ppermute | solution.py:510
  5.8 2.6 %collective-permute-start.1 = (bf16[144,128]{1,0:T(8,128)(2,1)S(1)}, bf16[144,128]{1,0:T(8,128)(2,1)S(1)}, u32[]{:S(2)}, u32[]{:S(2)}) collective-permute-start(bf16[144,128]{1,0:T(8,128)(2,1)S(1)} %pack.1), channel_id=1, source_target_pairs={{0,2},{1,3},{2,0},{3,1},{4,6},{5,7},{6,4},{7,5},{8,10},{9,11},{10,... | collective-permute-start | bytes 110600 | tf_op jit(solution)/shard_map/ppermute | solution.py:510
  8.4 1.3 %collective-permute-start.2 = (bf16[144,128]{1,0:T(8,128)(2,1)S(1)}, bf16[144,128]{1,0:T(8,128)(2,1)S(1)}, u32[]{:S(2)}, u32[]{:S(2)}) collective-permute-start(bf16[144,128]{1,0:T(8,128)(2,1)S(1)} %pack.1), channel_id=1, source_target_pairs={{0,3},{1,0},{2,1},{3,2},{4,7},{5,4},{6,5},{7,6},{8,11},{9,8},{10,9... | collective-permute-start | bytes 110600 | tf_op jit(solution)/shard_map/ppermute | solution.py:510
  9.7 0.8 %constant_dynamic-update-slice_fusion.3 = bf16[8,128,128]{2,1,0:T(8,128)(2,1)S(1)} fusion(bf16[2,128,128]{2,1,0:T(8,128)(2,1)} %param.18), kind=kLoop, calls=%fused_computation.21 | loop fusion | bytes 131072
  10.5 0.9 %constant_dynamic-update-slice_fusion.2 = bf16[8,128,128]{2,1,0:T(8,128)(2,1)S(1)} fusion(bf16[8,128,128]{2,1,0:T(8,128)(2,1)S(1)} %constant_dynamic-update-slice_fusion.3, bf16[2,128,128]{2,1,0:T(8,128)(2,1)} %param.19), kind=kLoop, calls=%fused_computation.20 | loop fusion | bytes 131072
  11.4 0.9 %constant_dynamic-update-slice_fusion.1 = bf16[8,128,128]{2,1,0:T(8,128)(2,1)S(1)} fusion(bf16[8,128,128]{2,1,0:T(8,128)(2,1)S(1)} %constant_dynamic-update-slice_fusion.2, bf16[2,128,128]{2,1,0:T(8,128)(2,1)} %param.20), kind=kLoop, calls=%fused_computation.19 | loop fusion | bytes 131072
  12.3 0.0 collective-permute-done
  12.3 0.0 collective-permute-done.1
  12.3 0.0 collective-permute-done.2
  12.3 0.1 collective-permute-start.3
  12.4 0.9 %constant_dynamic-update-slice_fusion.weight_all_ref = bf16[8,128,128]{2,1,0:T(8,128)(2,1)S(1)} fusion(bf16[8,128,128]{2,1,0:T(8,128)(2,1)S(1)} %constant_dynamic-update-slice_fusion.1, bf16[2,128,128]{2,1,0:T(8,128)(2,1)} %param.21), kind=kLoop, calls=%fused_computation.18 | loop fusion | bytes 131072 | tf_op jit(solution)/shard_map/concatenate | solution.py:536
  13.3 1.5 %collective-permute-start.4 = (bf16[4,144,128]{2,1,0:T(8,128)(2,1)S(1)}, bf16[4,144,128]{2,1,0:T(8,128)(2,1)S(1)}, u32[]{:S(2)}, u32[]{:S(2)}) collective-permute-start(bf16[4,144,128]{2,1,0:T(8,128)(2,1)S(1)} %pad_maximum_fusion.geo_a.state_a), channel_id=1, source_target_pairs={{0,8},{4,12},{8,16},{12,20},{16,24},{20,28},{24,0},{28,4},{1,9},{5... | collective-permute-start | bytes 442376 | tf_op jit(solution)/shard_map/ppermute | solution.py:510
  14.8 2.4 %collective-permute-start.5 = (bf16[4,144,128]{2,1,0:T(8,128)(2,1)S(1)}, bf16[4,144,128]{2,1,0:T(8,128)(2,1)S(1)}, u32[]{:S(2)}, u32[]{:S(2)}) collective-permute-start(bf16[4,144,128]{2,1,0:T(8,128)(2,1)S(1)} %pad_maximum_fusion.geo_a.state_a), channel_id=1, source_target_pairs={{0,12},{4,16},{8,20},{12,24},{16,28},{20,0},{24,4},{28,8},{1,13},{... | collective-permute-start | bytes 442376 | tf_op jit(solution)/shard_map/ppermute | solution.py:510
  17.2 0.5 collective-permute-start.6
  17.7 0.1 collective-permute-start.7
  17.8 0.1 collective-permute-done.3.geo_b.state_b
  18.0 1.5 %collective-permute-start.8 = (bf16[4,144,128]{2,1,0:T(8,128)(2,1)S(1)}, bf16[4,144,128]{2,1,0:T(8,128)(2,1)S(1)}, u32[]{:S(2)}, u32[]{:S(2)}) collective-permute-start(bf16[4,144,128]{2,1,0:T(8,128)(2,1)S(1)} %pad_maximum_fusion.geo_a.state_a), channel_id=1, source_target_pairs={{0,24},{4,28},{8,0},{12,4},{16,8},{20,12},{24,16},{28,20},{1,25},{... | collective-permute-start | bytes 442376 | tf_op jit(solution)/shard_map/ppermute | solution.py:510
  19.5 1.1 %collective-permute-done.4 = bf16[4,144,128]{2,1,0:T(8,128)(2,1)S(1)} collective-permute-done((bf16[4,144,128]{2,1,0:T(8,128)(2,1)S(1)}, bf16[4,144,128]{2,1,0:T(8,128)(2,1)S(1)}, u32[]{:S(2)}, u32[]{:S(2)}) %collective-permute-start.4) | collective-permute-done | bytes 147488 | tf_op jit(solution)/shard_map/ppermute | solution.py:510
  20.6 1.8 %collective-permute-start.9 = (bf16[4,144,128]{2,1,0:T(8,128)(2,1)S(1)}, bf16[4,144,128]{2,1,0:T(8,128)(2,1)S(1)}, u32[]{:S(2)}, u32[]{:S(2)}) collective-permute-start(bf16[4,144,128]{2,1,0:T(8,128)(2,1)S(1)} %pad_maximum_fusion.geo_a.state_a), channel_id=1, source_target_pairs={{0,28},{4,0},{8,4},{12,8},{16,12},{20,16},{24,20},{28,24},{1,29},{... | collective-permute-start | bytes 442376 | tf_op jit(solution)/shard_map/ppermute | solution.py:510
  22.4 3.3 %collective-permute-done.5 = bf16[4,144,128]{2,1,0:T(8,128)(2,1)S(1)} collective-permute-done((bf16[4,144,128]{2,1,0:T(8,128)(2,1)S(1)}, bf16[4,144,128]{2,1,0:T(8,128)(2,1)S(1)}, u32[]{:S(2)}, u32[]{:S(2)}) %collective-permute-start.5) | collective-permute-done | bytes 147488 | tf_op jit(solution)/shard_map/ppermute | solution.py:510
  25.7 0.2 collective-permute-done.6
  25.9 2.1 %collective-permute-done.7 = bf16[4,144,128]{2,1,0:T(8,128)(2,1)S(1)} collective-permute-done((bf16[4,144,128]{2,1,0:T(8,128)(2,1)S(1)}, bf16[4,144,128]{2,1,0:T(8,128)(2,1)S(1)}, u32[]{:S(2)}, u32[]{:S(2)}) %collective-permute-start.7) | collective-permute-done | bytes 147488 | tf_op jit(solution)/shard_map/ppermute | solution.py:510
  28.1 0.0 copy-start.1
  28.1 0.0 copy-start.3
  28.1 0.0 copy-start.4
  28.1 0.0 copy-start.5
  28.1 0.0 copy-start.6
  28.1 7.2 %conv.2.refs_4_ = f32[128,128]{1,0:T(8,128)S(1)} custom-call(bf16[4,144,128]{2,1,0:T(8,128)(2,1)S(1)} %pad_maximum_fusion.geo_a.state_a, bf16[4,144,128]{2,1,0:T(8,128)(2,1)S(1)} %collective-permute-done.3.geo_b.state_b, bf16[4,144,128]{2,1,0:T(8,128)(2,1)S(1)} %collective-permute-done.9.geo_c.state_c, ...), custom_call_target="tpu_custom_call" | custom-call | flops 40000000000 | bytes 2000000 | tf_op jit(solution)/shard_map/conv/pallas_call | solution.py:633
  35.4 6.5 %ewald.2 = (bf16[128,128]{1,0:T(8,128)(2,1)S(1)}, s32[40,128]{1,0:T(8,128)S(1)}, bf16[1024,128]{1,0:T(8,128)(2,1)S(1)}, bf16[16,1024,256]{2,1,0:T(8,128)(2,1)S(1)}) custom-call(s32[3,512]{1,0:T(4,128)S(1)} %copy-done.5, f32[2,128]{1,0:T(2,128)S(1)} %copy-done.6, bf16[8,4,144,128]{3,2,1,0:T(8,128)(2,1)S(1)} %bitcast_dynamic-update-slice_fusion.refs_2_, ...), custom_call_target="tpu_custom_call" | custom-call | flops 30000001024 | bytes 4000000 | tf_op jit(solution)/shard_map/ewald/pallas_call | solution.py:606
  41.9 0.7 collective-permute-start.10
  42.6 3.1 %collective-permute-start.11 = (bf16[128,128]{1,0:T(8,128)(2,1)S(1)}, bf16[128,128]{1,0:T(8,128)(2,1)S(1)}, u32[]{:S(2)}, u32[]{:S(2)}) collective-permute-start(bf16[128,128]{1,0:T(8,128)(2,1)S(1)} %get-tuple-element.12.refs_6_), channel_id=1, source_target_pairs={{0,2},{1,3},{2,0},{3,1},{4,6},{5,7},{6,4},{7,5},{8,10},{9,11},{10,... | collective-permute-start | bytes 98312 | tf_op jit(solution)/shard_map/ppermute | solution.py:510
  45.7 0.2 collective-permute-start.12
  45.9 2.3 %collective-permute-done.10 = bf16[128,128]{1,0:T(8,128)(2,1)S(1)} collective-permute-done((bf16[128,128]{1,0:T(8,128)(2,1)S(1)}, bf16[128,128]{1,0:T(8,128)(2,1)S(1)}, u32[]{:S(2)}, u32[]{:S(2)}) %collective-permute-start.10) | collective-permute-done | bytes 32800 | tf_op jit(solution)/shard_map/ppermute | solution.py:510
  48.2 1.2 %collective-permute-done.11 = bf16[128,128]{1,0:T(8,128)(2,1)S(1)} collective-permute-done((bf16[128,128]{1,0:T(8,128)(2,1)S(1)}, bf16[128,128]{1,0:T(8,128)(2,1)S(1)}, u32[]{:S(2)}, u32[]{:S(2)}) %collective-permute-start.11) | collective-permute-done | bytes 32800 | tf_op jit(solution)/shard_map/ppermute | solution.py:510
  49.3 0.4 collective-permute-done.12
  49.7 0.1 collective-permute-start.13
  49.8 3.2 %collective-permute-start.19 = (bf16[4,128,128]{2,1,0:T(8,128)(2,1)S(1)}, bf16[4,128,128]{2,1,0:T(8,128)(2,1)S(1)}, u32[]{:S(2)}, u32[]{:S(2)}) collective-permute-start(bf16[4,128,128]{2,1,0:T(8,128)(2,1)S(1)} %pad_maximum_fusion.1.state_a), channel_id=1, source_target_pairs={{0,28},{4,0},{8,4},{12,8},{16,12},{20,16},{24,20},{28,24},{1,29},{... | collective-permute-start | bytes 393224 | tf_op jit(solution)/shard_map/ppermute | solution.py:510
  53.0 1.6 %collective-permute-start.14 = (bf16[4,128,128]{2,1,0:T(8,128)(2,1)S(1)}, bf16[4,128,128]{2,1,0:T(8,128)(2,1)S(1)}, u32[]{:S(2)}, u32[]{:S(2)}) collective-permute-start(bf16[4,128,128]{2,1,0:T(8,128)(2,1)S(1)} %pad_maximum_fusion.1.state_a), channel_id=1, source_target_pairs={{0,8},{4,12},{8,16},{12,20},{16,24},{20,28},{24,0},{28,4},{1,9},{5... | collective-permute-start | bytes 393224 | tf_op jit(solution)/shard_map/ppermute | solution.py:510
  54.5 0.1 collective-permute-start.15
  54.7 1.1 %collective-permute-start.16 = (bf16[4,128,128]{2,1,0:T(8,128)(2,1)S(1)}, bf16[4,128,128]{2,1,0:T(8,128)(2,1)S(1)}, u32[]{:S(2)}, u32[]{:S(2)}) collective-permute-start(bf16[4,128,128]{2,1,0:T(8,128)(2,1)S(1)} %pad_maximum_fusion.1.state_a), channel_id=1, source_target_pairs={{0,16},{4,20},{8,24},{12,28},{16,0},{20,4},{24,8},{28,12},{1,17},{... | collective-permute-start | bytes 393224 | tf_op jit(solution)/shard_map/ppermute | solution.py:510
  55.7 1.3 %collective-permute-start.17 = (bf16[4,128,128]{2,1,0:T(8,128)(2,1)S(1)}, bf16[4,128,128]{2,1,0:T(8,128)(2,1)S(1)}, u32[]{:S(2)}, u32[]{:S(2)}) collective-permute-start(bf16[4,128,128]{2,1,0:T(8,128)(2,1)S(1)} %pad_maximum_fusion.1.state_a), channel_id=1, source_target_pairs={{0,20},{4,24},{8,28},{12,0},{16,4},{20,8},{24,12},{28,16},{1,21},{... | collective-permute-start | bytes 393224 | tf_op jit(solution)/shard_map/ppermute | solution.py:510
  57.0 1.7 %collective-permute-start.18 = (bf16[4,128,128]{2,1,0:T(8,128)(2,1)S(1)}, bf16[4,128,128]{2,1,0:T(8,128)(2,1)S(1)}, u32[]{:S(2)}, u32[]{:S(2)}) collective-permute-start(bf16[4,128,128]{2,1,0:T(8,128)(2,1)S(1)} %pad_maximum_fusion.1.state_a), channel_id=1, source_target_pairs={{0,24},{4,28},{8,0},{12,4},{16,8},{20,12},{24,16},{28,20},{1,25},{... | collective-permute-start | bytes 393224 | tf_op jit(solution)/shard_map/ppermute | solution.py:510
  58.7 7.2 %conv.3.refs_7_ = f32[128,128]{1,0:T(8,128)S(1)} custom-call(bf16[4,144,128]{2,1,0:T(8,128)(2,1)S(1)} %pad_maximum_fusion.geo_a.state_a, bf16[4,144,128]{2,1,0:T(8,128)(2,1)S(1)} %collective-permute-done.3.geo_b.state_b, bf16[4,144,128]{2,1,0:T(8,128)(2,1)S(1)} %collective-permute-done.9.geo_c.state_c, bf16[4,128,128]{2,1,0:T(8,128)(2,1)S(1)} %pad_maximum_fusion.1.state_a, ...), custom_call_target="tpu_custom_call" | custom-call | flops 40000000000 | bytes 2000000 | tf_op jit(solution)/shard_map/conv/pallas_call | solution.py:633
  66.2 4.2 %ewald.3 = bf16[128,128]{1,0:T(8,128)(2,1)} custom-call(s32[40,128]{1,0:T(8,128)S(1)} %get-tuple-element.9.refs_0_, bf16[1024,128]{1,0:T(8,128)(2,1)S(1)} %get-tuple-element.10.refs_1_, bf16[16,1024,256]{2,1,0:T(8,128)(2,1)S(1)} %get-tuple-element.11.refs_2_, s32[3,512]{1,0:T(4,128)S(1)} %copy-done.5, f32[2,128]{1,0:T(2,128)S(1)} %copy-done.6, ...), custom_call_target="tpu_custom_call" | custom-call | flops 30000001024 | bytes 4000000 | tf_op jit(solution)/shard_map/ewald/pallas_call | solution.py:606
  (34 shorter events, 0.4 us)
Async XLA Ops:
  0.7 0.8 %copy-start = (bf16[1,1,128,128]{3,2,1,0:T(8,128)(2,1)S(1)}, bf16[1,1,128,128]{3,2,1,0:T(8,128)(2,1)}, u32[]{:S(2)}) copy-start(bf16[1,1,128,128]{3,2,1,0:T(8,128)(2,1)} %features_ref.1) | copy-start | bytes 98308
  1.4 0.7 copy-start.2
  2.7 9.6 %collective-permute-start = (bf16[144,128]{1,0:T(8,128)(2,1)S(1)}, bf16[144,128]{1,0:T(8,128)(2,1)S(1)}, u32[]{:S(2)}, u32[]{:S(2)}) collective-permute-start(bf16[144,128]{1,0:T(8,128)(2,1)S(1)} %pack.1), channel_id=1, source_target_pairs={{0,1},{1,2},{2,3},{3,0},{4,5},{5,6},{6,7},{7,4},{8,9},{9,10},{10,1... | collective-permute-start | bytes 110600 | tf_op jit(solution)/shard_map/ppermute | solution.py:510
  5.8 6.5 %collective-permute-start.1 = (bf16[144,128]{1,0:T(8,128)(2,1)S(1)}, bf16[144,128]{1,0:T(8,128)(2,1)S(1)}, u32[]{:S(2)}, u32[]{:S(2)}) collective-permute-start(bf16[144,128]{1,0:T(8,128)(2,1)S(1)} %pack.1), channel_id=1, source_target_pairs={{0,2},{1,3},{2,0},{3,1},{4,6},{5,7},{6,4},{7,5},{8,10},{9,11},{10,... | collective-permute-start | bytes 110600 | tf_op jit(solution)/shard_map/ppermute | solution.py:510
  8.4 4.0 %collective-permute-start.2 = (bf16[144,128]{1,0:T(8,128)(2,1)S(1)}, bf16[144,128]{1,0:T(8,128)(2,1)S(1)}, u32[]{:S(2)}, u32[]{:S(2)}) collective-permute-start(bf16[144,128]{1,0:T(8,128)(2,1)S(1)} %pack.1), channel_id=1, source_target_pairs={{0,3},{1,0},{2,1},{3,2},{4,7},{5,4},{6,5},{7,6},{8,11},{9,8},{10,9... | collective-permute-start | bytes 110600 | tf_op jit(solution)/shard_map/ppermute | solution.py:510
  12.3 5.6 %collective-permute-start.3 = (bf16[4,144,128]{2,1,0:T(8,128)(2,1)S(1)}, bf16[4,144,128]{2,1,0:T(8,128)(2,1)S(1)}, u32[]{:S(2)}, u32[]{:S(2)}) collective-permute-start(bf16[4,144,128]{2,1,0:T(8,128)(2,1)S(1)} %pad_maximum_fusion.geo_a.state_a), channel_id=1, source_target_pairs={{0,4},{4,8},{8,12},{12,16},{16,20},{20,24},{24,28},{28,0},{1,5},{5... | collective-permute-start | bytes 442376 | tf_op jit(solution)/shard_map/ppermute | solution.py:510
  13.3 7.3 %collective-permute-start.4 = (bf16[4,144,128]{2,1,0:T(8,128)(2,1)S(1)}, bf16[4,144,128]{2,1,0:T(8,128)(2,1)S(1)}, u32[]{:S(2)}, u32[]{:S(2)}) collective-permute-start(bf16[4,144,128]{2,1,0:T(8,128)(2,1)S(1)} %pad_maximum_fusion.geo_a.state_a), channel_id=1, source_target_pairs={{0,8},{4,12},{8,16},{12,20},{16,24},{20,28},{24,0},{28,4},{1,9},{5... | collective-permute-start | bytes 442376 | tf_op jit(solution)/shard_map/ppermute | solution.py:510
  14.8 10.9 %collective-permute-start.5 = (bf16[4,144,128]{2,1,0:T(8,128)(2,1)S(1)}, bf16[4,144,128]{2,1,0:T(8,128)(2,1)S(1)}, u32[]{:S(2)}, u32[]{:S(2)}) collective-permute-start(bf16[4,144,128]{2,1,0:T(8,128)(2,1)S(1)} %pad_maximum_fusion.geo_a.state_a), channel_id=1, source_target_pairs={{0,12},{4,16},{8,20},{12,24},{16,28},{20,0},{24,4},{28,8},{1,13},{... | collective-permute-start | bytes 442376 | tf_op jit(solution)/shard_map/ppermute | solution.py:510
  17.2 8.6 %collective-permute-start.6 = (bf16[4,144,128]{2,1,0:T(8,128)(2,1)S(1)}, bf16[4,144,128]{2,1,0:T(8,128)(2,1)S(1)}, u32[]{:S(2)}, u32[]{:S(2)}) collective-permute-start(bf16[4,144,128]{2,1,0:T(8,128)(2,1)S(1)} %pad_maximum_fusion.geo_a.state_a), channel_id=1, source_target_pairs={{0,16},{4,20},{8,24},{12,28},{16,0},{20,4},{24,8},{28,12},{1,17},{... | collective-permute-start | bytes 442376 | tf_op jit(solution)/shard_map/ppermute | solution.py:510
  17.7 10.2 %collective-permute-start.7 = (bf16[4,144,128]{2,1,0:T(8,128)(2,1)S(1)}, bf16[4,144,128]{2,1,0:T(8,128)(2,1)S(1)}, u32[]{:S(2)}, u32[]{:S(2)}) collective-permute-start(bf16[4,144,128]{2,1,0:T(8,128)(2,1)S(1)} %pad_maximum_fusion.geo_a.state_a), channel_id=1, source_target_pairs={{0,20},{4,24},{8,28},{12,0},{16,4},{20,8},{24,12},{28,16},{1,21},{... | collective-permute-start | bytes 442376 | tf_op jit(solution)/shard_map/ppermute | solution.py:510
  18.0 10.0 %collective-permute-start.8 = (bf16[4,144,128]{2,1,0:T(8,128)(2,1)S(1)}, bf16[4,144,128]{2,1,0:T(8,128)(2,1)S(1)}, u32[]{:S(2)}, u32[]{:S(2)}) collective-permute-start(bf16[4,144,128]{2,1,0:T(8,128)(2,1)S(1)} %pad_maximum_fusion.geo_a.state_a), channel_id=1, source_target_pairs={{0,24},{4,28},{8,0},{12,4},{16,8},{20,12},{24,16},{28,20},{1,25},{... | collective-permute-start | bytes 442376 | tf_op jit(solution)/shard_map/ppermute | solution.py:510
  20.6 7.4 %collective-permute-start.9 = (bf16[4,144,128]{2,1,0:T(8,128)(2,1)S(1)}, bf16[4,144,128]{2,1,0:T(8,128)(2,1)S(1)}, u32[]{:S(2)}, u32[]{:S(2)}) collective-permute-start(bf16[4,144,128]{2,1,0:T(8,128)(2,1)S(1)} %pad_maximum_fusion.geo_a.state_a), channel_id=1, source_target_pairs={{0,28},{4,0},{8,4},{12,8},{16,12},{20,16},{24,20},{28,24},{1,29},{... | collective-permute-start | bytes 442376 | tf_op jit(solution)/shard_map/ppermute | solution.py:510
  28.1 7.3 %copy-start.1 = (bf16[1,1,128,128]{3,2,1,0:T(8,128)(2,1)S(1)}, bf16[1,1,128,128]{3,2,1,0:T(8,128)(2,1)}, u32[]{:S(2)}) copy-start(bf16[1,1,128,128]{3,2,1,0:T(8,128)(2,1)} %features_ref.1) | copy-start | bytes 98308
  28.1 7.3 %copy-start.3 = (bf16[2,128,128]{2,1,0:T(8,128)(2,1)S(1)}, bf16[2,128,128]{2,1,0:T(8,128)(2,1)}, u32[]{:S(2)}) copy-start(bf16[2,128,128]{2,1,0:T(8,128)(2,1)} %refs_8_.1) | copy-start | bytes 196612
  28.1 7.3 %copy-start.4 = (bf16[2,128,128]{2,1,0:T(8,128)(2,1)S(1)}, bf16[2,128,128]{2,1,0:T(8,128)(2,1)}, u32[]{:S(2)}) copy-start(bf16[2,128,128]{2,1,0:T(8,128)(2,1)} %refs_9_.1) | copy-start | bytes 196612
  28.1 7.3 %copy-start.5 = (s32[3,512]{1,0:T(4,128)S(1)}, s32[3,512]{1,0:T(4,128)}, u32[]{:S(2)}) copy-start(s32[3,512]{1,0:T(4,128)} %refs_3_.1) | copy-start | bytes 18436
  28.1 7.3 %copy-start.6 = (f32[2,128]{1,0:T(2,128)S(1)}, f32[2,128]{1,0:T(2,128)}, u32[]{:S(2)}) copy-start(f32[2,128]{1,0:T(2,128)} %refs_4_.1) | copy-start | bytes 3076
  41.9 6.2 %collective-permute-start.10 = (bf16[128,128]{1,0:T(8,128)(2,1)S(1)}, bf16[128,128]{1,0:T(8,128)(2,1)S(1)}, u32[]{:S(2)}, u32[]{:S(2)}) collective-permute-start(bf16[128,128]{1,0:T(8,128)(2,1)S(1)} %get-tuple-element.12.refs_6_), channel_id=1, source_target_pairs={{0,1},{1,2},{2,3},{3,0},{4,5},{5,6},{6,7},{7,4},{8,9},{9,10},{10,1... | collective-permute-start | bytes 98312 | tf_op jit(solution)/shard_map/ppermute | solution.py:510
  42.6 6.7 %collective-permute-start.11 = (bf16[128,128]{1,0:T(8,128)(2,1)S(1)}, bf16[128,128]{1,0:T(8,128)(2,1)S(1)}, u32[]{:S(2)}, u32[]{:S(2)}) collective-permute-start(bf16[128,128]{1,0:T(8,128)(2,1)S(1)} %get-tuple-element.12.refs_6_), channel_id=1, source_target_pairs={{0,2},{1,3},{2,0},{3,1},{4,6},{5,7},{6,4},{7,5},{8,10},{9,11},{10,... | collective-permute-start | bytes 98312 | tf_op jit(solution)/shard_map/ppermute | solution.py:510
  45.7 4.0 %collective-permute-start.12 = (bf16[128,128]{1,0:T(8,128)(2,1)S(1)}, bf16[128,128]{1,0:T(8,128)(2,1)S(1)}, u32[]{:S(2)}, u32[]{:S(2)}) collective-permute-start(bf16[128,128]{1,0:T(8,128)(2,1)S(1)} %get-tuple-element.12.refs_6_), channel_id=1, source_target_pairs={{0,3},{1,0},{2,1},{3,2},{4,7},{5,4},{6,5},{7,6},{8,11},{9,8},{10,9... | collective-permute-start | bytes 98312 | tf_op jit(solution)/shard_map/ppermute | solution.py:510
  49.7 6.0 %collective-permute-start.13 = (bf16[4,128,128]{2,1,0:T(8,128)(2,1)S(1)}, bf16[4,128,128]{2,1,0:T(8,128)(2,1)S(1)}, u32[]{:S(2)}, u32[]{:S(2)}) collective-permute-start(bf16[4,128,128]{2,1,0:T(8,128)(2,1)S(1)} %pad_maximum_fusion.1.state_a), channel_id=1, source_target_pairs={{0,4},{4,8},{8,12},{12,16},{16,20},{20,24},{24,28},{28,0},{1,5},{5... | collective-permute-start | bytes 393224 | tf_op jit(solution)/shard_map/ppermute | solution.py:510
  49.8 7.2 %collective-permute-start.19 = (bf16[4,128,128]{2,1,0:T(8,128)(2,1)S(1)}, bf16[4,128,128]{2,1,0:T(8,128)(2,1)S(1)}, u32[]{:S(2)}, u32[]{:S(2)}) collective-permute-start(bf16[4,128,128]{2,1,0:T(8,128)(2,1)S(1)} %pad_maximum_fusion.1.state_a), channel_id=1, source_target_pairs={{0,28},{4,0},{8,4},{12,8},{16,12},{20,16},{24,20},{28,24},{1,29},{... | collective-permute-start | bytes 393224 | tf_op jit(solution)/shard_map/ppermute | solution.py:510
  53.0 13.0 %collective-permute-start.14 = (bf16[4,128,128]{2,1,0:T(8,128)(2,1)S(1)}, bf16[4,128,128]{2,1,0:T(8,128)(2,1)S(1)}, u32[]{:S(2)}, u32[]{:S(2)}) collective-permute-start(bf16[4,128,128]{2,1,0:T(8,128)(2,1)S(1)} %pad_maximum_fusion.1.state_a), channel_id=1, source_target_pairs={{0,8},{4,12},{8,16},{12,20},{16,24},{20,28},{24,0},{28,4},{1,9},{5... | collective-permute-start | bytes 393224 | tf_op jit(solution)/shard_map/ppermute | solution.py:510
  54.5 11.5 %collective-permute-start.15 = (bf16[4,128,128]{2,1,0:T(8,128)(2,1)S(1)}, bf16[4,128,128]{2,1,0:T(8,128)(2,1)S(1)}, u32[]{:S(2)}, u32[]{:S(2)}) collective-permute-start(bf16[4,128,128]{2,1,0:T(8,128)(2,1)S(1)} %pad_maximum_fusion.1.state_a), channel_id=1, source_target_pairs={{0,12},{4,16},{8,20},{12,24},{16,28},{20,0},{24,4},{28,8},{1,13},{... | collective-permute-start | bytes 393224 | tf_op jit(solution)/shard_map/ppermute | solution.py:510
  54.7 11.4 %collective-permute-start.16 = (bf16[4,128,128]{2,1,0:T(8,128)(2,1)S(1)}, bf16[4,128,128]{2,1,0:T(8,128)(2,1)S(1)}, u32[]{:S(2)}, u32[]{:S(2)}) collective-permute-start(bf16[4,128,128]{2,1,0:T(8,128)(2,1)S(1)} %pad_maximum_fusion.1.state_a), channel_id=1, source_target_pairs={{0,16},{4,20},{8,24},{12,28},{16,0},{20,4},{24,8},{28,12},{1,17},{... | collective-permute-start | bytes 393224 | tf_op jit(solution)/shard_map/ppermute | solution.py:510
  55.7 10.4 %collective-permute-start.17 = (bf16[4,128,128]{2,1,0:T(8,128)(2,1)S(1)}, bf16[4,128,128]{2,1,0:T(8,128)(2,1)S(1)}, u32[]{:S(2)}, u32[]{:S(2)}) collective-permute-start(bf16[4,128,128]{2,1,0:T(8,128)(2,1)S(1)} %pad_maximum_fusion.1.state_a), channel_id=1, source_target_pairs={{0,20},{4,24},{8,28},{12,0},{16,4},{20,8},{24,12},{28,16},{1,21},{... | collective-permute-start | bytes 393224 | tf_op jit(solution)/shard_map/ppermute | solution.py:510
  57.0 9.1 %collective-permute-start.18 = (bf16[4,128,128]{2,1,0:T(8,128)(2,1)S(1)}, bf16[4,128,128]{2,1,0:T(8,128)(2,1)S(1)}, u32[]{:S(2)}, u32[]{:S(2)}) collective-permute-start(bf16[4,128,128]{2,1,0:T(8,128)(2,1)S(1)} %pad_maximum_fusion.1.state_a), channel_id=1, source_target_pairs={{0,24},{4,28},{8,0},{12,4},{16,8},{20,12},{24,16},{28,20},{1,25},{... | collective-permute-start | bytes 393224 | tf_op jit(solution)/shard_map/ppermute | solution.py:510
